TPU v7x, 64 devices: a 2x2x8 block of a 4x4x8 slice. The times are simulated.
64 devices in a mesh: dp: 4 (over x, y), tp: 16 (over z, core).
Axes of the slice: x: 2, y: 2, z: 8, core: 2. Of those that a mesh axis runs over, the one named last changes fastest.
The devices are a block of a 4x4x8 slice.
Arguments:
- hidden: bfloat16 [4, 2048, 2560], P('dp'), parts along dimension 0
- grad_out: bfloat16 [4, 2048, 2560], P('dp'), parts along dimension 0
- norm_gain: bfloat16 [2560], replicated
- w_query: bfloat16 [2560, 4096], P(None, 'tp')
- w_key: bfloat16 [2560, 1024], replicated
- w_value: bfloat16 [2560, 1024], replicated
- w_out: bfloat16 [4096, 2560], P('tp')
Outputs:
- output 1: bfloat16 [4, 2048, 2560], P('dp'), parts along dimension 0
- output 2: bfloat16 [4, 2048, 2560], P('dp'), parts along dimension 0
- output 3: float32 [10240], P('dp'), parts along dimension 0
- output 4: float32 [10240, 4096], P('dp', 'tp'), parts along dimension 0
- output 5: float32 [10240, 2048], P('dp', 'tp'), parts along dimension 0
- output 6: float32 [10240, 2048], P('dp', 'tp'), parts along dimension 0
- output 7: float32 [16384, 2560], P(('dp', 'tp')), parts along dimension 0
There are 4 independent parts. A program takes and returns all parts, laid end to end along the dimension named above; an argument that names none is the same for every part.
All inputs are finite; a program needn't handle non-finite values.
Results may differ from a plain program's by a relative error of at most 0.0098541.
Values sent between devices are 32-bit elements.
A program may use at most 768 MiB of HBM per device.

v0:
```python
import math
import jax
import jax.numpy as jnp
from jax import lax
from jax.sharding import PartitionSpec as P

HEAD_DIM = 128
NORM_EPS = 1.0e-5
ROPE_BASE = 10000.0
MASK_VALUE = -1.0e30
SCORE_SCALE = 1.0 / math.sqrt(HEAD_DIM)


def rope_tables(seq_len):
    positions = jnp.arange(seq_len, dtype=jnp.float32)
    inv_freq = ROPE_BASE ** (-jnp.arange(0, HEAD_DIM, 2, dtype=jnp.float32) / HEAD_DIM)
    angles = positions[:, None] * inv_freq[None, :]
    return jnp.cos(angles), jnp.sin(angles)


def rotate_pairs(tensor, cos_t, sin_t):
    pair_view = tensor.reshape(tensor.shape[:-1] + (HEAD_DIM // 2, 2))
    even_part = pair_view[..., 0]
    odd_part = pair_view[..., 1]
    cos_b = cos_t[:, None, :]
    sin_b = sin_t[:, None, :]
    rotated = jnp.stack([even_part * cos_b - odd_part * sin_b, even_part * sin_b + odd_part * cos_b], axis=-1)
    return rotated.reshape(tensor.shape)


def group_sum(tensor, tp_size, group_size):
    total = tensor
    for level in range(group_size.bit_length() - 1):
        distance = 2 ** level
        partner_pairs = [(source, source ^ distance) for source in range(tp_size)]
        total = total + lax.ppermute(total, 'tp', perm=partner_pairs)
    return total


def solution(mesh):
    tp_size = mesh.shape['tp']

    def block_fn(hidden, grad_out, norm_gain, w_query, w_key, w_value, w_out):
        kv_heads = w_key.shape[1] // HEAD_DIM
        group_size = tp_size // kv_heads
        q_heads_local = w_query.shape[1] // HEAD_DIM
        batch_local, seq_len, d_model = hidden.shape
        kv_index = lax.axis_index('tp') // group_size
        w_kv = jnp.concatenate([
            lax.dynamic_slice_in_dim(w_key, kv_index * HEAD_DIM, HEAD_DIM, axis=1),
            lax.dynamic_slice_in_dim(w_value, kv_index * HEAD_DIM, HEAD_DIM, axis=1)], axis=1)
        cos_t, sin_t = rope_tables(seq_len)

        hidden_f32 = hidden.astype(jnp.float32)
        inv_rms = lax.rsqrt(jnp.mean(hidden_f32 * hidden_f32, axis=-1, keepdims=True) + NORM_EPS)
        unit_rows = hidden_f32 * inv_rms
        gain_f32 = norm_gain.astype(jnp.float32)
        normed = (unit_rows * gain_f32).astype(jnp.bfloat16)
        q_proj = jnp.einsum('bsd,de->bse', normed, w_query, preferred_element_type=jnp.float32)
        q_rot = rotate_pairs(q_proj.reshape(batch_local, seq_len, q_heads_local, HEAD_DIM), cos_t, sin_t).astype(jnp.bfloat16)
        kv_proj = jnp.einsum('bsd,de->bse', normed, w_kv, preferred_element_type=jnp.float32)
        k_rot = rotate_pairs(kv_proj[:, :, None, :HEAD_DIM], cos_t, sin_t)[:, :, 0, :].astype(jnp.bfloat16)
        v_head = kv_proj[:, :, HEAD_DIM:].astype(jnp.bfloat16)
        scores = jnp.einsum('bqjh,bkh->bjqk', q_rot, k_rot, preferred_element_type=jnp.float32) * SCORE_SCALE
        causal = jnp.arange(seq_len)[:, None] >= jnp.arange(seq_len)[None, :]
        attn_probs = jax.nn.softmax(jnp.where(causal, scores, MASK_VALUE), axis=-1)
        probs_bf16 = attn_probs.astype(jnp.bfloat16)
        attn_heads = jnp.einsum('bjqk,bkh->bqjh', probs_bf16, v_head, preferred_element_type=jnp.float32).astype(jnp.bfloat16)
        attn_flat = attn_heads.reshape(batch_local, seq_len, q_heads_local * HEAD_DIM)
        out_part = jnp.einsum('bse,ed->bsd', attn_flat, w_out, preferred_element_type=jnp.float32)
        attn_sum = lax.psum(out_part, 'tp')
        block_out = (hidden_f32 + attn_sum).astype(jnp.bfloat16)

        grad_w_out = jnp.einsum('bse,bsd->ed', attn_flat, grad_out, preferred_element_type=jnp.float32)
        grad_heads = jnp.einsum('bsd,ed->bse', grad_out, w_out, preferred_element_type=jnp.float32).astype(jnp.bfloat16).reshape(batch_local, seq_len, q_heads_local, HEAD_DIM)
        grad_probs = jnp.einsum('bqjh,bkh->bjqk', grad_heads, v_head, preferred_element_type=jnp.float32)
        grad_v = jnp.einsum('bjqk,bqjh->bkh', probs_bf16, grad_heads, preferred_element_type=jnp.float32)
        row_dot = jnp.sum(attn_probs * grad_probs, axis=-1, keepdims=True)
        grad_scores = (attn_probs * (grad_probs - row_dot) * SCORE_SCALE).astype(jnp.bfloat16)
        grad_q_rot = jnp.einsum('bjqk,bkh->bqjh', grad_scores, k_rot, preferred_element_type=jnp.float32)
        grad_k_rot = jnp.einsum('bjqk,bqjh->bkh', grad_scores, q_rot, preferred_element_type=jnp.float32)
        grad_q = rotate_pairs(grad_q_rot, cos_t, -sin_t).astype(jnp.bfloat16).reshape(batch_local, seq_len, q_heads_local * HEAD_DIM)
        grad_k = rotate_pairs(grad_k_rot[:, :, None, :], cos_t, -sin_t)[:, :, 0, :]
        grad_kv = jnp.concatenate([grad_k, grad_v], axis=-1).astype(jnp.bfloat16)
        grad_w_query = jnp.einsum('bsd,bse->de', normed, grad_q, preferred_element_type=jnp.float32)
        grad_w_kv_part = jnp.einsum('bsd,bse->de', normed, grad_kv, preferred_element_type=jnp.float32)
        grad_normed_part = (jnp.einsum('bse,de->bsd', grad_q, w_query, preferred_element_type=jnp.float32)
                            + jnp.einsum('bse,de->bsd', grad_kv, w_kv, preferred_element_type=jnp.float32))
        grad_normed = lax.psum(grad_normed_part, 'tp')
        gain_grad_rows = grad_normed * gain_f32
        grad_hidden = (grad_out.astype(jnp.float32) + inv_rms * (gain_grad_rows - unit_rows * jnp.mean(gain_grad_rows * unit_rows, axis=-1, keepdims=True))).astype(jnp.bfloat16)
        grad_gain = jnp.sum(grad_normed * unit_rows, axis=(0, 1))
        grad_w_kv = group_sum(grad_w_kv_part, tp_size, group_size)
        return block_out, grad_hidden, grad_gain, grad_w_query, grad_w_kv[:, :HEAD_DIM], grad_w_kv[:, HEAD_DIM:], grad_w_out

    act_spec = P('dp', None, None)
    return jax.shard_map(
        block_fn, mesh=mesh,
        in_specs=(act_spec, act_spec, P(None), P(None, 'tp'), P(None, None), P(None, None), P('tp', None)),
        out_specs=(act_spec, act_spec, P('dp'), P('dp', 'tp'), P('dp', 'tp'), P('dp', 'tp'), P(('dp', 'tp'), None)),
        check_vma=False)
```

profile of v0, /device:TPU:21, one launch (start us, length us, event | category | flops | bytes accessed | tf_op | source)
XLA Modules:
  0.0 748.2 jit_solution(14462632839289797811)
XLA Ops:
  7.2 0.0 copy-start
  7.2 0.1 all-reduce.3.cloned.1.call-start
  7.3 4.1 iota_compare_fusion
  11.4 6.1 fusion.18
  17.5 0.7 convert_element_type.115
  18.2 1.4 constant_dynamic-slice_fusion
  19.6 0.0 copy-start.9
  19.7 0.8 copy-done.9
  20.5 6.6 fusion.41
  27.1 0.0 copy-start.20
  27.1 1.3 copy-done.20
  28.4 1.0 slice.50
  29.5 2.8 reshape_broadcast_in_dim.4
  32.3 2.6 fusion.91
  34.9 3.0 fusion.79
  37.9 2.4 subtract_convert_fusion.1
  40.4 0.1 pad_maximum_fusion.6
  40.4 0.5 copy.27
  41.0 1.0 convert_element_type.117
  42.0 1.6 copy.28
  43.6 4.0 dot_general.68
  47.5 0.0 copy-start.1
  47.5 6.4 fusion.47
  54.0 0.3 multiply_subtract_fusion.1
  54.4 0.1 maximum_convert_fusion
  54.5 1.1 copy.76
  55.6 0.0 copy-start.17
  55.6 14.8 %fusion.10 = (f32[2,2048]{1,0:T(2,128)S(1)}, f32[2048,2048,2]{1,0,2:T(8,128)}) fusion(pred[2048,2048]{0,1:T(8,128)(4,1)S(1)} %copy-done.1, bf16[2048,2,128]{0,1,2:T(2,128)(2,1)S(1)} %bitcast.161, bf16[2048,128]{0,1:T(8,128)(2,1)S(1)} %copy-done.22), kind=kOutput, calls=%fused_computation.17 | convolution fusion | flops 2172645376 | bytes 39337984 | tf_op jit(solution)/shard_map/bqjh,bkh->bjqk/dot_general | solution.py:64
  70.4 14.7 %fusion.9 = f32[2,2048]{1,0:T(2,128)S(1)} fusion(f32[2048,2048,2]{1,0,2:T(8,128)} %get-tuple-element.33, f32[2,2048]{1,0:T(2,128)S(1)} %get-tuple-element.32, pred[2048,2048]{0,1:T(8,128)(4,1)S(1)} %copy-done.1), kind=kLoop, calls=%fused_computation.16 | loop fusion | flops 33550336 | bytes 37781504 | tf_op jit(solution)/shard_map/reduce_sum | solution.py:66
  85.1 0.0 copy-start.21
  85.1 7.0 fusion.50
  92.2 25.7 %fusion = (f32[2,2048]{1,0:T(2,128)S(1)}, f32[2048,2048,2]{1,0,2:T(8,128)}) fusion(f32[2,2048]{1,0:T(2,128)S(1)} %fusion.9, f32[2,2048]{1,0:T(2,128)S(1)} %get-tuple-element.32, f32[2048,2048,2]{1,0,2:T(8,128)} %get-tuple-element.33, pred[2048,2048]{0,1:T(8,128)(4,1)S(1)} %copy-done.1, bf16[2048,2,128]{0,2,1:T(8,128)(2,1)S(1)} %bitcast.163, ...), kind=kOutput, calls=%fused_computation.3 | convolution fusion | flops 2197811200 | bytes 72925184 | tf_op jit(solution)/shard_map/bqjh,bkh->bjqk/dot_general | solution.py:76
  117.9 17.1 %fusion.62 = bf16[2048,128]{0,1:T(8,128)(2,1)} fusion(bf16[2048,2,128]{0,2,1:T(8,128)(2,1)S(1)} %bitcast.164, f32[2,2048]{1,0:T(2,128)S(1)} %fusion.9, f32[2,2048]{1,0:T(2,128)S(1)} %get-tuple-element.32, f32[2048,2048,2]{1,0,2:T(8,128)} %get-tuple-element.33, pred[2048,2048]{0,1:T(8,128)(4,1)} %iota_compare_fusion), kind=kOutput, calls=%fused_computation.58 | convolution fusion | flops 2189688832 | bytes 39354368 | tf_op jit(solution)/shard_map/bjqk,bqjh->bkh/dot_general | solution.py:77
  135.0 1.0 reshape.507
  136.0 18.4 %fusion.53 = bf16[128,2,2048]{2,0,1:T(8,128)(2,1)} fusion(f32[1,2048,256]{1,2,0:T(8,128)} %copy-done.20, f32[2,2048]{1,0:T(2,128)S(1)} %fusion.9, f32[2,2048]{1,0:T(2,128)S(1)} %get-tuple-element.32, f32[2048,2048,2]{1,0,2:T(8,128)} %get-tuple-element.33, pred[2048,2048]{0,1:T(8,128)(4,1)} %iota_compare_fusion), kind=kOutput, calls=%fused_computation.55 | convolution fusion | flops 2189950976 | bytes 39354368 | tf_op jit(solution)/shard_map/bjqk,bkh->bqjh/dot_general | solution.py:68
  154.5 29.9 %fusion.3 = bf16[1,2,2048,2048]{2,3,1,0:T(8,128)(2,1)} fusion(f32[2048,2048,2]{1,0,2:T(8,128)} %get-tuple-element.35, f32[2,2048]{1,0:T(2,128)S(1)} %get-tuple-element.34, f32[2,2048]{1,0:T(2,128)S(1)} %fusion.9, f32[2,2048]{1,0:T(2,128)S(1)} %get-tuple-element.32, f32[2048,2048,2]{1,0,2:T(8,128)} %get-tuple-element.33, pred[2048,2048]{0,1:T(8,128)(4,1)} %iota_compare_fusion), kind=kLoop, calls=%fused_computation.6 | loop fusion | flops 67108864 | bytes 88129536 | tf_op jit(solution)/shard_map/convert_element_type | solution.py:79
  184.4 11.7 %fusion.59 = f32[1,2048,1,64,2]{1,3,4,2,0:T(8,128)S(1)} fusion(bf16[1,2,2048,2048]{2,3,1,0:T(8,128)(2,1)} %fusion.3, bf16[64,2,2,2048]{3,2,1,0:T(2,128)(2,1)S(1)} %bitcast.162), kind=kOutput, calls=%fused_computation.57 | convolution fusion | flops 2147483648 | bytes 18874368 | tf_op jit(solution)/shard_map/bjqk,bqjh->bkh/dot_general | solution.py:81
  196.1 2.8 subtract_convert_fusion
  198.9 0.1 pad_maximum_fusion.7
  199.0 0.5 copy.42
  199.5 1.0 concatenate.33
  200.5 8.4 %fusion.44 = f32[1,2048,2,128]{1,3,2,0:T(8,128)S(1)} fusion(bf16[2048,128,1]{0,1,2:T(8,128)(2,1)} %reshape.507, bf16[1,2,2048,2048]{2,3,1,0:T(8,128)(2,1)} %fusion.3), kind=kOutput, calls=%fused_computation.52 | convolution fusion | flops 2147483648 | bytes 19398656 | tf_op jit(solution)/shard_map/bjqk,bkh->bqjh/dot_general | solution.py:80
  208.9 1.6 copy.37
  210.5 0.2 fusion.90
  210.7 2.2 multiply_subtract_fusion
  212.9 0.1 maximum_convert_fusion.1
  213.0 2.0 copy.40
  215.1 2.2 convert_element_type.129
  217.3 10.0 %fusion.92 = f32[2048,2560]{1,0:T(8,128)} fusion(bf16[2048,256]{0,1:T(8,128)(2,1)} %convert_element_type.129, bf16[2560,256]{1,0:T(8,128)(2,1)S(1)} %copy-done.3), kind=kOutput, calls=%fused_computation.101 | convolution fusion | flops 2684354560 | bytes 23330816 | tf_op jit(solution)/shard_map/bse,de->bsd/dot_general | solution.py:87
  227.3 8.7 %convolution_bitcast_fusion = f32[1,2048,2560]{2,1,0:T(8,128)} fusion(bf16[2048,256]{0,1:T(8,128)(2,1)S(1)} %bitcast.159, bf16[256,2560]{1,0:T(8,128)(2,1)S(1)} %copy-done), kind=kOutput, calls=%fused_computation.37 | convolution fusion | flops 2684354560 | bytes 23330816 | tf_op jit(solution)/shard_map/bse,ed->bsd/dot_general | solution.py:70
  236.1 13.6 %add_bitcast_fusion = f32[1,2048,2560]{2,1,0:T(8,128)} fusion(f32[2048,2560]{1,0:T(8,128)} %fusion.92, bf16[2560,128]{1,0:T(8,128)(2,1)S(1)} %copy-done.10, bf16[2560,128]{1,0:T(8,128)(2,1)S(1)} %copy-done.12, bf16[2048,128]{0,1:T(8,128)(2,1)S(1)} %copy-done.19, bf16[2048,128]{0,1:T(8,128)(2,1)S(1)} %copy-done.13), kind=kOutput, calls=%fused_computation.27 | convolution fusion | flops 2694316032 | bytes 44302336 | tf_op jit(solution)/shard_map/bse,de->bsd/dot_general | solution.py:88
  249.7 0.1 all-reduce.3.cloned.1.call-update
  249.8 0.6 copy-done.24
  250.4 0.0 copy-done.26
  250.4 8.2 %fusion.36 = f32[2560,256]{1,0:T(8,128)S(1)} fusion(bf16[2048,128]{0,1:T(8,128)(2,1)S(1)} %copy-done.19, bf16[2048,128]{0,1:T(8,128)(2,1)S(1)} %copy-done.13, bf16[1,2048,2560]{2,1,0:T(8,128)(2,1)} %param.7, f32[2560]{0:T(1024)S(1)} %copy-done.24, f32[2048]{0:T(1024)S(1)} %copy-done.26), kind=kOutput, calls=%fused_computation.46 | convolution fusion | flops 2707423232 | bytes 14174208 | tf_op jit(solution)/shard_map/bsd,bse->de/dot_general | solution.py:86
  258.6 0.0 slice-start.2
  258.6 4.8 collective-permute-start
  263.4 8.4 %fusion.30 = f32[256,2560]{1,0:T(8,128)} fusion(bf16[2048,256]{0,1:T(8,128)(2,1)S(1)} %bitcast.160, bf16[1,2048,2560]{2,1,0:T(8,128)(2,1)} %param.8), kind=kOutput, calls=%fused_computation.40 | convolution fusion | flops 2684354560 | bytes 14155776 | tf_op jit(solution)/shard_map/bse,bsd->ed/dot_general | solution.py:74
  271.8 6.0 fusion.34
  277.8 0.3 add.70
  278.2 1.7 fusion.89
  279.8 420.0 %all-reduce.3.cloned.1.call-done = (f32[1,2048,2560]{2,1,0:T(8,128)}, f32[1,2048,2560]{2,1,0:T(8,128)}) async-done(((f32[1,2048,2560]{2,1,0:T(8,128)}, f32[1,2048,2560]{2,1,0:T(8,128)}), (f32[1,2048,2560]{2,1,0:T(8,128)}, f32[1,2048,2560]{2,1,0:T(8,128)})) %all-reduce.3.cloned.1.call-update) | async-done | bytes 41943056 | tf_op jit(solution)/shard_map/psum | solution.py:71
  699.9 14.7 %fusion.17 = (f32[2560]{0:T(1024)}, f32[2048]{0:T(1024)S(1)}) fusion(f32[1,2048,2560]{2,1,0:T(8,128)} %get-tuple-element.10, bf16[1,2048,2560]{2,1,0:T(8,128)(2,1)} %param.7, f32[2048]{0:T(1024)S(1)} %copy-done.26, f32[2560]{0:T(1024)S(1)} %copy-done.24), kind=kLoop, calls=%fused_computation.24 | loop fusion | flops 36695552 | bytes 31494144 | tf_op jit(solution)/shard_map/reduce_sum | solution.py:92
  714.6 26.6 %fusion.16 = (bf16[1,2048,2560]{2,1,0:T(8,128)(2,1)}, bf16[1,2048,2560]{2,1,0:T(8,128)(2,1)}) fusion(bf16[1,2048,2560]{2,1,0:T(8,128)(2,1)S(1)} %bitcast.156, bf16[1,2048,2560]{2,1,0:T(8,128)(2,1)} %param.8, f32[1,2048,2560]{2,1,0:T(8,128)} %get-tuple-element.10, f32[2048]{0:T(1024)S(1)} %broadcast_multiply_fusion, f32[2560]{0:T(1024)S(1)} %copy-done.24, ...), kind=kLoop, calls=%fused_computation.23 | loop fusion | flops 57671680 | bytes 83912704 | tf_op jit(solution)/shard_map/convert_element_type | solution.py:91
  (65 shorter events, 0.1 us)
Async XLA Ops:
  7.2 77.9 %copy-start = (bf16[256,2560]{1,0:T(8,128)(2,1)S(1)}, bf16[256,2560]{1,0:T(8,128)(2,1)}, u32[]{:S(2)}) copy-start(bf16[256,2560]{1,0:T(8,128)(2,1)} %param.13) | copy-start | bytes 3932164
  7.2 692.7 %all-reduce.3.cloned.1.call-start = ((), (), s32[]{:S(2)}) async-start(), calls=%async_computation | async-start | bytes 83886080 | tf_op jit(solution)/shard_map/psum | solution.py:71
  7.3 30.6 %copy-start.27 = (f32[64]{0:T(128)}, f32[64]{0:T(128)S(1)}, u32[]{:S(2)}) copy-start(f32[64]{0:T(128)S(1)} %multiply_power_fusion) | copy-start | bytes 772
  17.5 30.0 %copy-start.25 = (f32[2048]{0:T(1024)}, f32[2048]{0:T(1024)S(1)}, u32[]{:S(2)}) copy-start(f32[2048]{0:T(1024)S(1)} %add_rsqrt_fusion) | copy-start | bytes 24580
  18.2 29.3 %copy-start.23 = (f32[2560]{0:T(1024)}, f32[2560]{0:T(1024)S(1)}, u32[]{:S(2)}) copy-start(f32[2560]{0:T(1024)S(1)} %convert_element_type.115) | copy-start | bytes 30724
  19.6 0.8 copy-start.9
  19.6 7.5 copy-start.11
  20.5 21.5 %copy-start.2 = (bf16[2560,256]{1,0:T(8,128)(2,1)S(1)}, bf16[2560,256]{1,0:T(8,128)(2,1)}, u32[]{:S(2)}) copy-start(bf16[2560,256]{1,0:T(8,128)(2,1)} %param.10) | copy-start | bytes 3932164
  27.1 1.3 copy-start.20
  41.0 13.0 %copy-start.4 = (bf16[1,2048,1,64,2]{1,4,3,2,0:T(2,128)(2,1)}, bf16[1,2048,1,64,2]{1,4,3,2,0:T(2,128)(2,1)S(1)}, u32[]{:S(2)}) copy-start(bf16[1,2048,1,64,2]{1,4,3,2,0:T(2,128)(2,1)S(1)} %copy.27) | copy-start | bytes 1572868
  47.5 6.5 copy-start.6
  47.5 6.5 copy-start.14
  47.5 8.0 %copy-start.1 = (pred[2048,2048]{0,1:T(8,128)(4,1)S(1)}, pred[2048,2048]{0,1:T(8,128)(4,1)}, u32[]{:S(2)}) copy-start(pred[2048,2048]{0,1:T(8,128)(4,1)} %iota_compare_fusion) | copy-start | bytes 12582916
  47.5 8.0 %copy-start.22 = (bf16[2048,128]{0,1:T(8,128)(2,1)S(1)}, bf16[2048,128]{0,1:T(8,128)(2,1)}, u32[]{:S(2)}) copy-start(bf16[2048,128]{0,1:T(8,128)(2,1)} %convert_element_type.117) | copy-start | bytes 1572868
  55.6 14.9 %copy-start.17 = (bf16[1,2048,2,64,2]{1,2,4,3,0:T(2,128)(2,1)}, bf16[1,2048,2,64,2]{1,2,4,3,0:T(2,128)(2,1)S(1)}, u32[]{:S(2)}) copy-start(bf16[1,2048,2,64,2]{1,2,4,3,0:T(2,128)(2,1)S(1)} %copy.76) | copy-start | bytes 3145732
  85.1 7.0 copy-start.21
  117.9 17.1 %copy-start.5 = (bf16[1,2048,1,64,2]{1,4,3,2,0:T(2,128)(2,1)S(1)}, bf16[1,2048,1,64,2]{1,4,3,2,0:T(2,128)(2,1)}, u32[]{:S(2)}) copy-start(bf16[1,2048,1,64,2]{1,4,3,2,0:T(2,128)(2,1)} %copy-done.4) | copy-start | bytes 1572868
  154.5 29.9 %copy-start.18 = (bf16[1,2048,2,64,2]{1,2,4,3,0:T(2,128)(2,1)S(1)}, bf16[1,2048,2,64,2]{1,2,4,3,0:T(2,128)(2,1)}, u32[]{:S(2)}) copy-start(bf16[1,2048,2,64,2]{1,2,4,3,0:T(2,128)(2,1)} %copy-done.17) | copy-start | bytes 3145732
  184.4 11.7 %copy-start.28 = (f32[64]{0:T(128)S(1)}, f32[64]{0:T(128)}, u32[]{:S(2)}) copy-start(f32[64]{0:T(128)} %copy-done.27) | copy-start | bytes 772
  198.9 11.8 %copy-start.7 = (f32[2048,64]{0,1:T(8,128)S(1)}, f32[2048,64]{0,1:T(8,128)}, u32[]{:S(2)}) copy-start(f32[2048,64]{0,1:T(8,128)} %get-tuple-element.31) | copy-start | bytes 1572868
  200.5 16.8 %copy-start.3 = (bf16[2560,256]{1,0:T(8,128)(2,1)S(1)}, bf16[2560,256]{1,0:T(8,128)(2,1)}, u32[]{:S(2)}) copy-start(bf16[2560,256]{1,0:T(8,128)(2,1)} %param.10) | copy-start | bytes 3932164
  217.3 10.0 %copy-start.15 = (bf16[128,2,2048]{2,0,1:T(8,128)(2,1)S(1)}, bf16[128,2,2048]{2,0,1:T(8,128)(2,1)}, u32[]{:S(2)}) copy-start(bf16[128,2,2048]{2,0,1:T(8,128)(2,1)} %fusion.53) | copy-start | bytes 3145732
  227.3 8.8 %copy-start.10 = (bf16[2560,128]{1,0:T(8,128)(2,1)S(1)}, bf16[2560,128]{1,0:T(8,128)(2,1)}, u32[]{:S(2)}) copy-start(bf16[2560,128]{1,0:T(8,128)(2,1)} %copy-done.9) | copy-start | bytes 1966084
  227.3 8.8 %copy-start.12 = (bf16[2560,128]{1,0:T(8,128)(2,1)S(1)}, bf16[2560,128]{1,0:T(8,128)(2,1)}, u32[]{:S(2)}) copy-start(bf16[2560,128]{1,0:T(8,128)(2,1)} %copy-done.11) | copy-start | bytes 1966084
  227.3 8.8 %copy-start.13 = (bf16[2048,128]{0,1:T(8,128)(2,1)S(1)}, bf16[2048,128]{0,1:T(8,128)(2,1)}, u32[]{:S(2)}) copy-start(bf16[2048,128]{0,1:T(8,128)(2,1)} %concatenate.33) | copy-start | bytes 1572868
  227.3 8.8 %copy-start.19 = (bf16[2048,128]{0,1:T(8,128)(2,1)S(1)}, bf16[2048,128]{0,1:T(8,128)(2,1)}, u32[]{:S(2)}) copy-start(bf16[2048,128]{0,1:T(8,128)(2,1)} %fusion.62) | copy-start | bytes 1572868
  249.7 0.7 copy-start.24
  249.7 0.7 copy-start.26
  250.4 13.0 %copy-start.16 = (bf16[128,2,2048]{2,0,1:T(8,128)(2,1)S(1)}, bf16[128,2,2048]{2,0,1:T(8,128)(2,1)}, u32[]{:S(2)}) copy-start(bf16[128,2,2048]{2,0,1:T(8,128)(2,1)} %fusion.53) | copy-start | bytes 3145732
  250.4 21.4 %slice-start = ((s8[10485760]{0:T(1024)(128)(4,1)}), s8[4194304]{0:T(1024)(128)(4,1)S(1)}, s32[]{:S(2)}) async-start(s8[10485760]{0:T(1024)(128)(4,1)} %bitcast.153), calls=%async_computation.1 | async-start | bytes 8388608
  250.4 21.4 %slice-start.1 = ((s8[10485760]{0:T(1024)(128)(4,1)}), s8[4194304]{0:T(1024)(128)(4,1)S(1)}, s32[]{:S(2)}) async-start(s8[10485760]{0:T(1024)(128)(4,1)} %bitcast.153), calls=%async_computation.2 | async-start | bytes 8388608
  258.6 13.1 %slice-start.2 = ((s8[10485760]{0:T(1024)(128)(4,1)}), s8[2097152]{0:T(1024)(128)(4,1)S(1)}, s32[]{:S(2)}) async-start(s8[10485760]{0:T(1024)(128)(4,1)} %bitcast.153), calls=%async_computation.3 | async-start | bytes 4194304
  258.6 13.1 %copy-start.8 = (bf16[2048,256]{0,1:T(8,128)(2,1)S(1)}, bf16[2048,256]{0,1:T(8,128)(2,1)}, u32[]{:S(2)}) copy-start(bf16[2048,256]{0,1:T(8,128)(2,1)} %convert_element_type.129) | copy-start | bytes 3145732
  258.6 19.2 %collective-permute-start = (f32[2560,256]{1,0:T(8,128)S(1)}, f32[2560,256]{1,0:T(8,128)S(1)}, u32[]{:S(2)}, u32[]{:S(2)}) collective-permute-start(f32[2560,256]{1,0:T(8,128)S(1)} %fusion.36), channel_id=1, source_target_pairs={{0,1},{1,0},{2,3},{3,2},{4,5},{5,4},{6,7},{7,6},{8,9},{9,8},{10,11... | collective-permute-start | bytes 7864328 | tf_op jit(solution)/shard_map/ppermute | solution.py:36
  279.8 434.7 %slice-start.3 = ((s8[10485760]{0:T(1024)(128)(4,1)}), s8[2097152]{0:T(1024)(128)(4,1)S(1)}, s32[]{:S(2)}) async-start(s8[10485760]{0:T(1024)(128)(4,1)} %bitcast.155), calls=%async_computation.4 | async-start | bytes 4194304
  699.9 14.7 %slice-start.4 = ((s8[10485760]{0:T(1024)(128)(4,1)}), s8[4194304]{0:T(1024)(128)(4,1)S(1)}, s32[]{:S(2)}) async-start(s8[10485760]{0:T(1024)(128)(4,1)} %bitcast.155), calls=%async_computation.5 | async-start | bytes 8388608
  699.9 14.7 %slice-start.5 = ((s8[10485760]{0:T(1024)(128)(4,1)}), s8[4194304]{0:T(1024)(128)(4,1)S(1)}, s32[]{:S(2)}) async-start(s8[10485760]{0:T(1024)(128)(4,1)} %bitcast.155), calls=%async_computation.6 | async-start | bytes 8388608
Sparse Core Ops, SparseCore 0:
  249.9 449.9 all-reduce.2
where the time goes:
time: 752 us; the launch traced here: 748 us
  waiting for transfers between devices  420 us (56%)
  matrix products  171 us (23%)
  other arithmetic  108 us (14%)
  local copies, waits for them, and re-layouts  29.2 us (4%)
  between operations  14.7 us (2%)
    psum x1, waiting for transfers between devices, block_fn(): attn_sum = lax.psum(out_part, 'tp')  420 us
    convert_element_type x1, other arithmetic, block_fn(): (attn_probs * (grad_probs - row_dot) * SCORE_SCALE).astype(jnp.bfloat16)  29.9 us
    convert_element_type x1, other arithmetic, block_fn(): (grad_out.astype(jnp.float32) + inv_rms * (gain_grad_rows - unit_rows * j...  26.6 us
    dot_general x1, matrix products, block_fn(): jnp.einsum('bqjh,bkh->bjqk', grad_heads, v_head, preferred_element_type=j...  25.7 us
    dot_general x1, matrix products, block_fn(): jnp.einsum('bjqk,bkh->bqjh', probs_bf16, v_head, preferred_element_type=j...  18.4 us
    dot_general x1, matrix products, block_fn(): jnp.einsum('bjqk,bqjh->bkh', probs_bf16, grad_heads, preferred_element_ty...  17.1 us
  transfers between devices with their start and end apart: 2, of which 1 were waited for; matrix products, arithmetic and copies ran while one was open for 3% of the time, Pallas kernels for 0%

commit v1 on v0

v1 whole, which is shorter than its diff:
```python
import math
import jax
import jax.numpy as jnp
import numpy as np
from jax import lax
from jax.experimental import pallas as pl
from jax.experimental.pallas import tpu as pltpu
from jax.sharding import PartitionSpec as P

HEAD_DIM = 128
NORM_EPS = 1.0e-5
ROPE_BASE = 10000.0
MASK_VALUE = -1.0e30
SCORE_SCALE = 1.0 / math.sqrt(HEAD_DIM)
EXP2_SCALE = SCORE_SCALE * math.log2(math.e)
ROWS = 256
BF16 = jnp.bfloat16
F32 = jnp.float32


def dot(a, b, contract):
    return lax.dot_general(a, b, ((contract[:1], contract[1:]), ((), ())), preferred_element_type=F32)


def rope_tables(seq_len):
    inv_freq = ROPE_BASE ** (-np.arange(0, HEAD_DIM, 2, dtype=np.float64) / HEAD_DIM)
    angles = np.arange(seq_len, dtype=np.float64)[:, None] * inv_freq[None, :]
    cos_t = np.repeat(np.cos(angles), 2, axis=1)
    sin_t = np.stack([-np.sin(angles), np.sin(angles)], axis=-1).reshape(seq_len, HEAD_DIM)
    return cos_t.astype(np.float32), sin_t.astype(np.float32)


def rotate(t, cos_t, sin_t):
    even = lax.broadcasted_iota(jnp.int32, t.shape, 1) % 2 == 0
    swapped = jnp.where(even, pltpu.roll(t, HEAD_DIM - 1, 1), pltpu.roll(t, 1, 1))
    return t * cos_t + swapped * sin_t


def proj_kernel(x_ref, dout_ref, gain_ref, wqkv_ref, wo_ref, cos_ref, sin_ref, n_ref, q_ref, k_ref, v_ref, do_ref):
    x = x_ref[...].astype(F32)
    inv = lax.rsqrt(jnp.mean(x * x, axis=-1, keepdims=True) + NORM_EPS)
    n = (x * inv * gain_ref[...]).astype(BF16)
    n_ref[...] = n
    qkv = dot(n, wqkv_ref[...], (1, 0))
    cos_t, sin_t = cos_ref[...], sin_ref[...]
    q_ref[:, :HEAD_DIM] = rotate(qkv[:, :HEAD_DIM], cos_t, sin_t).astype(BF16)
    q_ref[:, HEAD_DIM:] = rotate(qkv[:, HEAD_DIM:2 * HEAD_DIM], cos_t, sin_t).astype(BF16)
    k_ref[...] = rotate(qkv[:, 2 * HEAD_DIM:3 * HEAD_DIM], cos_t, sin_t).astype(BF16)
    v_ref[...] = qkv[:, 3 * HEAD_DIM:].astype(BF16)
    do_ref[...] = dot(dout_ref[...], wo_ref[...], (1, 1)).astype(BF16)


def project(x, dout, gain, wqkv, wo, cos_t, sin_t):
    seq, d = x.shape
    row = lambda w: pl.BlockSpec((ROWS, w), lambda i: (i, 0))
    whole = lambda a: pl.BlockSpec(a.shape, lambda i: (0, 0))
    widths = (d, 2 * HEAD_DIM, HEAD_DIM, HEAD_DIM, 2 * HEAD_DIM)
    return pl.pallas_call(
        proj_kernel, grid=(seq // ROWS,),
        in_specs=[row(d), row(d), whole(gain), whole(wqkv), whole(wo), row(HEAD_DIM), row(HEAD_DIM)],
        out_specs=[row(w) for w in widths],
        out_shape=[jax.ShapeDtypeStruct((seq, w), BF16) for w in widths],
        cost_estimate=pl.CostEstimate(flops=2 * seq * d * 6 * HEAD_DIM, bytes_accessed=6 * seq * d, transcendentals=0),
        name='project')(x, dout, gain, wqkv, wo, cos_t, sin_t)


def stack_heads(ref, rows):
    return jnp.concatenate([ref[rows, :HEAD_DIM], ref[rows, HEAD_DIM:]], axis=0)


def attn_fwd_kernel(q_ref, k_ref, v_ref, o_ref):
    seq = q_ref.shape[0]
    row_id = lax.broadcasted_iota(jnp.int32, (2 * ROWS, ROWS), 0) % ROWS
    causal = row_id >= lax.broadcasted_iota(jnp.int32, (2 * ROWS, ROWS), 1)
    for i in range(seq // ROWS):
        lo = i * ROWS
        rows = pl.ds(lo, ROWS)
        q2 = stack_heads(q_ref, rows)
        s_diag = jnp.where(causal, dot(q2, k_ref[rows, :], (1, 1)), MASK_VALUE)
        m = jnp.max(s_diag, axis=-1, keepdims=True)
        if lo:
            s_pre = dot(q2, k_ref[:lo, :], (1, 1))
            m = jnp.maximum(m, jnp.max(s_pre, axis=-1, keepdims=True))
        p_diag = jnp.exp2((s_diag - m) * EXP2_SCALE)
        total = jnp.sum(p_diag, axis=-1, keepdims=True)
        if lo:
            p_pre = jnp.exp2((s_pre - m) * EXP2_SCALE)
            total = total + jnp.sum(p_pre, axis=-1, keepdims=True)
        scale = 1.0 / total
        o2 = dot((p_diag * scale).astype(BF16), v_ref[rows, :], (1, 0))
        if lo:
            o2 = o2 + dot((p_pre * scale).astype(BF16), v_ref[:lo, :], (1, 0))
        o_ref[rows, :HEAD_DIM] = o2[:ROWS].astype(BF16)
        o_ref[rows, HEAD_DIM:] = o2[ROWS:].astype(BF16)


def attn_fwd(q, k, v):
    seq = q.shape[0]
    return pl.pallas_call(
        attn_fwd_kernel,
        out_shape=jax.ShapeDtypeStruct(q.shape, BF16),
        compiler_params=pltpu.CompilerParams(vmem_limit_bytes=48 * 2**20),
        cost_estimate=pl.CostEstimate(flops=4 * seq * seq * HEAD_DIM, bytes_accessed=8 * seq * HEAD_DIM, transcendentals=seq * seq),
        name='attn_fwd')(q, k, v)


def attn_bwd_rows(i, q_ref, k_ref, v_ref, do_ref, cos_ref, sin_ref, dq_ref, dk_acc, dv_acc):
    lo, hi = i * ROWS, (i + 1) * ROWS
    rows = pl.ds(lo, ROWS)
    q2, do2 = stack_heads(q_ref, rows), stack_heads(do_ref, rows)
    k_all, v_all = k_ref[:hi, :], v_ref[:hi, :]
    key_id = lax.broadcasted_iota(jnp.int32, (ROWS, 2 * ROWS), 0)
    causal = key_id <= lax.broadcasted_iota(jnp.int32, (ROWS, 2 * ROWS), 1) % ROWS
    s_t = dot(k_all, q2, (1, 1))
    s_diag = jnp.where(causal, s_t[lo:], MASK_VALUE)
    s_t = jnp.concatenate([s_t[:lo], s_diag], axis=0) if lo else s_diag
    m = jnp.max(s_t, axis=0, keepdims=True)
    p = jnp.exp2((s_t - m) * EXP2_SCALE)
    p = p * (1.0 / jnp.sum(p, axis=0, keepdims=True))
    dp = dot(v_all, do2, (1, 1))
    delta = jnp.sum(p * dp, axis=0, keepdims=True)
    ds = (p * (dp - delta) * SCORE_SCALE).astype(BF16)
    dv = dot(p.astype(BF16), do2, (1, 0))
    dk = dot(ds, q2, (1, 0))
    dq2 = dot(ds, k_all, (0, 0))
    if lo:
        dk_acc[:lo, :] += dk[:lo]
        dv_acc[:lo, :] += dv[:lo]
    dk_acc[lo:hi, :] = dk[lo:]
    dv_acc[lo:hi, :] = dv[lo:]
    cos_t, sin_t = cos_ref[rows, :], sin_ref[rows, :]
    dq_ref[rows, :HEAD_DIM] = rotate(dq2[:ROWS], cos_t, -sin_t).astype(BF16)
    dq_ref[rows, HEAD_DIM:] = rotate(dq2[ROWS:], cos_t, -sin_t).astype(BF16)


def attn_bwd_kernel(q_ref, k_ref, v_ref, do_ref, cos_ref, sin_ref, dq_ref, dkv_ref, dk_acc):
    seq = q_ref.shape[0]
    dv_acc = dkv_ref.at[:, pl.ds(HEAD_DIM, HEAD_DIM)]
    for i in range(seq // ROWS):
        attn_bwd_rows(i, q_ref, k_ref, v_ref, do_ref, cos_ref, sin_ref, dq_ref, dk_acc, dv_acc)
    dkv_ref[:, :HEAD_DIM] = rotate(dk_acc[...], cos_ref[...], -sin_ref[...])


def attn_bwd(q, k, v, do, cos_t, sin_t):
    seq = q.shape[0]
    return pl.pallas_call(
        attn_bwd_kernel,
        out_shape=[jax.ShapeDtypeStruct(q.shape, BF16), jax.ShapeDtypeStruct((seq, 2 * HEAD_DIM), F32)],
        scratch_shapes=[pltpu.VMEM((seq, HEAD_DIM), F32)],
        compiler_params=pltpu.CompilerParams(vmem_limit_bytes=56 * 2**20),
        cost_estimate=pl.CostEstimate(flops=10 * seq * seq * HEAD_DIM, bytes_accessed=16 * seq * HEAD_DIM, transcendentals=seq * seq),
        name='attn_bwd')(q, k, v, do, cos_t, sin_t)


def group_sum(tensor, tp_size, group_size):
    total = tensor
    for level in range(group_size.bit_length() - 1):
        distance = 2 ** level
        partner_pairs = [(source, source ^ distance) for source in range(tp_size)]
        total = total + lax.ppermute(total, 'tp', perm=partner_pairs)
    return total


def solution(mesh):
    tp_size = mesh.shape['tp']

    def block_fn(hidden, grad_out, norm_gain, w_query, w_key, w_value, w_out):
        kv_heads = w_key.shape[1] // HEAD_DIM
        group_size = tp_size // kv_heads
        batch, seq_len, d_model = hidden.shape
        kv_index = lax.axis_index('tp') // group_size
        w_k = lax.dynamic_slice_in_dim(w_key, kv_index * HEAD_DIM, HEAD_DIM, axis=1)
        w_v = lax.dynamic_slice_in_dim(w_value, kv_index * HEAD_DIM, HEAD_DIM, axis=1)
        w_qkv = jnp.concatenate([w_query, w_k, w_v], axis=1)
        cos_t, sin_t = rope_tables(seq_len)
        x, dout = hidden[0], grad_out[0]
        gain = norm_gain.astype(F32)[None, :]

        n, q, k, v, do = project(x, dout, gain, w_qkv, w_out, cos_t, sin_t)
        o = attn_fwd(q, k, v)
        out_part = dot(o, w_out, (1, 0))
        attn_sum = lax.psum(out_part, 'tp')
        x32 = x.astype(F32)
        block_out = (x32 + attn_sum).astype(BF16)

        dq, dkv_part = attn_bwd(q, k, v, do, cos_t, sin_t)
        dkv = group_sum(dkv_part, tp_size, group_size)
        d_all = jnp.concatenate([dq, (dkv_part).astype(BF16)], axis=1)
        dn_part = dot(d_all, w_qkv, (1, 1))
        dn_part, attn_sum = lax.optimization_barrier((dn_part, attn_sum))
        dn = lax.psum(dn_part, 'tp')
        grad_w_out = dot(o, dout, (0, 0))
        grad_w_query = dot(n, dq, (0, 0))
        dkv = dkv.astype(BF16)
        grad_w_key = dot(n, dkv[:, :HEAD_DIM], (0, 0))
        grad_w_value = dot(n, dkv[:, HEAD_DIM:], (0, 0))
        inv = lax.rsqrt(jnp.mean(x32 * x32, axis=-1, keepdims=True) + NORM_EPS)
        unit = x32 * inv
        scaled = dn * gain
        grad_hidden = (dout.astype(F32) + inv * (scaled - unit * jnp.mean(scaled * unit, axis=-1, keepdims=True))).astype(BF16)
        grad_gain = jnp.sum(dn * unit, axis=0)
        return block_out[None], grad_hidden[None], grad_gain, grad_w_query, grad_w_key, grad_w_value, grad_w_out

    act_spec = P('dp', None, None)
    return jax.shard_map(
        block_fn, mesh=mesh,
        in_specs=(act_spec, act_spec, P(None), P(None, 'tp'), P(None, None), P(None, None), P('tp', None)),
        out_specs=(act_spec, act_spec, P('dp'), P('dp', 'tp'), P('dp', 'tp'), P('dp', 'tp'), P(('dp', 'tp'), None)),
        check_vma=False)
```

time: 752 us -> 589 us (0.78)
  matrix products: 171 us -> 42.5 us
  other arithmetic: 108 us -> 53.6 us
  Pallas kernels: 0 us -> 51.7 us
  local copies, waits for them, and re-layouts: 29.2 us -> 6.04 us
  waiting for transfers between devices: 420 us -> 406 us
    psum x1, waiting for transfers between devices: 420 us -> 193 us  [block_fn(): attn_sum = lax.psum(out_part, 'tp')]
    psum x0 -> x1, waiting for transfers between devices: none -> 209 us  [block_fn(): dn = lax.psum(dn_part, 'tp')]
    dot_general x15 -> x6, matrix products: 171 us -> 42.5 us  [dot(): lax.dot_general(a, b, ((contract[:1], contract[1:]), ((), ())), preferred...]
    convert_element_type x5 -> x2, other arithmetic: 57.4 us -> 2.68 us  [the longest x1 2.67 us: block_fn(): dkv = dkv.astype(BF16)]
    pallas_call x0 -> x3, Pallas kernels: none -> 51.7 us  [the longest x1 22.8 us: attn_bwd(): pl.pallas_call(attn_bwd_kernel, out_shape=[jax.ShapeDtypeStruct(q.shape,...]
    broadcast_in_dim x0 -> x1, other arithmetic: none -> 28.7 us  [block_fn(): grad_hidden[None]]
    reduce_sum x3 -> x2, other arithmetic: 35.4 us -> 19.2 us  [the longest x1 13 us: block_fn(): grad_gain = jnp.sum(dn * unit, axis=0)]
  transfers between devices with their start and end apart: 2 -> 3, of which waited for: 1 -> 3; matrix products, arithmetic and copies ran while one was open for 3% -> 7% of each run, Pallas kernels for 0% -> 4%
where the time goes in v1:
time: 589 us; the launch traced here: 580 us
  waiting for transfers between devices  406 us (69%)
  other arithmetic  53.6 us (9%)
  Pallas kernels  51.7 us (9%)
  matrix products  42.5 us (7%)
  between operations  14.7 us (2%)
  local copies, waits for them, and re-layouts  6.04 us (1%)
    psum x1, waiting for transfers between devices, block_fn(): dn = lax.psum(dn_part, 'tp')  209 us
    psum x1, waiting for transfers between devices, block_fn(): attn_sum = lax.psum(out_part, 'tp')  193 us
    dot_general x6, matrix products, dot(): lax.dot_general(a, b, ((contract[:1], contract[1:]), ((), ())), preferred...  42.5 us
    broadcast_in_dim x1, other arithmetic, block_fn(): grad_hidden[None]  28.7 us
    pallas_call x1, Pallas kernels, attn_bwd(): pl.pallas_call(attn_bwd_kernel, out_shape=[jax.ShapeDtypeStruct(q.shape,...  22.8 us
    pallas_call x1, Pallas kernels, project(): pl.pallas_call(proj_kernel, grid=(seq // ROWS,), in_specs=[row(d), row(d)...  19.5 us
    reduce_sum x1, other arithmetic, block_fn(): grad_gain = jnp.sum(dn * unit, axis=0)  13 us
  transfers between devices with their start and end apart: 3, of which 3 were waited for; matrix products, arithmetic and copies ran while one was open for 7% of the time, Pallas kernels for 4%

profile of v1, /device:TPU:21, one launch (start us, length us, event | category | flops | bytes accessed | tf_op | source)
XLA Modules:
  0.0 579.8 jit_solution(2888961008848531387)
XLA Ops:
  7.2 0.1 all-reduce.3.cloned.1.call-start
  7.3 1.3 broadcast_in_dim.11.gain_ref
  8.6 1.4 constant_dynamic-slice_fusion
  10.0 3.0 pad_maximum_fusion.wqkv_ref
  13.0 19.5 %project.1 = (bf16[2048,2560]{1,0:T(8,128)(2,1)}, bf16[2048,256]{1,0:T(8,128)(2,1)}, bf16[2048,128]{1,0:T(8,128)(2,1)}, bf16[2048,128]{1,0:T(8,128)(2,1)}, bf16[2048,256]{1,0:T(8,128)(2,1)}) custom-call(bf16[2048,2560]{1,0:T(8,128)(2,1)} %bitcast.21, bf16[2048,2560]{1,0:T(8,128)(2,1)} %bitcast.22, f32[1,2560]{1,0:T(1,128)} %broadcast_in_dim.11.gain_ref, ...), custom_call_target="tpu_custom_call" | custom-call | flops 8053063680 | bytes 31457280 | tf_op jit(solution)/shard_map/project/pallas_call | solution.py:58
  32.5 0.0 copy-start
  32.5 1.2 copy-done
  33.7 0.0 copy-start.1
  33.7 1.0 copy-done.1
  34.8 0.0 copy-start.2
  34.8 1.0 copy-done.2
  35.8 9.5 %attn_fwd.1 = bf16[2048,256]{1,0:T(8,128)(2,1)S(1)} custom-call(bf16[2048,256]{1,0:T(8,128)(2,1)S(1)} %copy-done, bf16[2048,128]{1,0:T(8,128)(2,1)S(1)} %copy-done.1, bf16[2048,128]{1,0:T(8,128)(2,1)S(1)} %copy-done.2), custom_call_target="tpu_custom_call" | custom-call | flops 2147483648 | bytes 2097152 | tf_op jit(solution)/shard_map/attn_fwd/pallas_call | solution.py:99
  45.3 9.8 %fusion.24 = f32[2048,2560]{1,0:T(8,128)} fusion(bf16[2048,256]{1,0:T(8,128)(2,1)S(1)} %attn_fwd.1, bf16[256,2560]{1,0:T(8,128)(2,1)} %wo_ref.1), kind=kOutput, calls=%fused_computation.33 | convolution fusion | flops 2684354560 | bytes 23330816 | tf_op jit(solution)/shard_map/dot_general | solution.py:22
  55.1 0.1 all-reduce.3.cloned.1.call-update
  55.2 0.5 all-reduce.5.cloned.1.call-start
  55.7 0.0 copy-start.3
  55.7 22.8 %attn_bwd.1 = (bf16[2048,256]{1,0:T(8,128)(2,1)}, f32[2048,256]{1,0:T(8,128)}) custom-call(bf16[2048,256]{1,0:T(8,128)(2,1)} %get-tuple-element.15.q_ref, bf16[2048,128]{1,0:T(8,128)(2,1)} %get-tuple-element.16.k_ref, bf16[2048,128]{1,0:T(8,128)(2,1)} %get-tuple-element.17.v_ref, bf16[2048,256]{1,0:T(8,128)(2,1)} %get-tuple-element.18.do_ref, ...), custom_call_target="tpu_custom_call" | custom-call | flops 5368709120 | bytes 4194304 | tf_op jit(solution)/shard_map/attn_bwd/pallas_call | solution.py:146
  78.5 4.7 collective-permute-start
  83.2 4.3 collective-permute-done
  87.4 2.7 add_convert_fusion
  90.1 0.0 copy-done.3
  90.1 11.5 %fusion.13 = f32[2048,2560]{1,0:T(8,128)} fusion(bf16[2048,256]{1,0:T(8,128)(2,1)S(1)} %get-tuple-element.28, bf16[2048,256]{1,0:T(8,128)(2,1)} %get-tuple-element.19, bf16[2560,128]{1,0:T(8,128)(2,1)S(1)} %get-tuple-element.29, bf16[2560,128]{1,0:T(8,128)(2,1)S(1)} %get-tuple-element.30, bf16[2560,256]{1,0:T(8,128)(2,1)S(1)} %copy-done.3), kind=kOutput, calls=%fused_computation.17 | convolution fusion | flops 5380767744 | bytes 25690112 | tf_op jit(solution)/shard_map/dot_general | solution.py:22
  101.6 0.0 copy-start.4
  101.6 193.0 %all-reduce.3.cloned.1.call-done = f32[2048,2560]{1,0:T(8,128)} async-done(((f32[2048,2560]{1,0:T(8,128)}), f32[2048,2560]{1,0:T(8,128)}) %all-reduce.3.cloned.1.call-update) | async-done | bytes 20971536 | tf_op jit(solution)/shard_map/psum | solution.py:182
  294.6 0.1 all-reduce.5.cloned.1.call-update
  294.7 0.0 copy-done.4
  294.7 0.0 slice-start
  294.7 0.0 slice-start.1
  294.7 6.2 %fusion.10 = f32[2048]{0:T(1024)S(1)} fusion(bf16[1,2048,2560]{2,1,0:T(8,128)(2,1)} %param.9), kind=kLoop, calls=%fused_computation.13 | loop fusion | flops 15726592 | bytes 10493952 | tf_op jit(solution)/shard_map/reduce_sum | solution.py:197
  300.9 0.0 copy-start.5
  301.0 0.0 slice-start.2
  301.0 8.5 %fusion.22 = f32[256,2560]{1,0:T(8,128)} fusion(bf16[2048,256]{1,0:T(8,128)(2,1)S(1)} %attn_fwd.1, bf16[1,2048,2560]{2,1,0:T(8,128)(2,1)} %param.10), kind=kOutput, calls=%fused_computation.31 | convolution fusion | flops 2684354560 | bytes 14155776 | tf_op jit(solution)/shard_map/dot_general | solution.py:22
  309.5 0.0 slice-done
  309.5 0.0 slice-done.1
  309.5 0.0 copy-done.5
  309.5 0.0 slice-done.2
  309.5 4.4 fusion.25
  314.0 4.0 fusion.17
  318.0 4.3 fusion.19
  322.2 208.7 %all-reduce.5.cloned.1.call-done = f32[2048,2560]{1,0:T(8,128)} async-done(((f32[2048,2560]{1,0:T(8,128)}), f32[2048,2560]{1,0:T(8,128)}) %all-reduce.5.cloned.1.call-update) | async-done | bytes 20971536 | tf_op jit(solution)/shard_map/psum | solution.py:191
  530.9 13.0 %fusion.8 = (f32[2560]{0:T(1024)}, f32[2048]{0:T(1024)S(1)}) fusion(f32[2048,2560]{1,0:T(8,128)} %all-reduce.5.cloned.1.call-done, f32[2048]{0:T(1024)S(1)} %add_rsqrt_fusion, bf16[1,2048,2560]{2,1,0:T(8,128)(2,1)} %param.9, f32[2560]{0:T(1024)S(1)} %convert_element_type.22), kind=kLoop, calls=%fused_computation.11 | loop fusion | flops 36695552 | bytes 31494144 | tf_op jit(solution)/shard_map/reduce_sum | solution.py:201
  543.9 28.7 %fusion.12 = (bf16[1,2048,2560]{2,1,0:T(8,128)(2,1)}, bf16[1,2048,2560]{2,1,0:T(8,128)(2,1)}) fusion(f32[2048,2560]{1,0:T(8,128)} %all-reduce.5.cloned.1.call-done, f32[2048]{0:T(1024)S(1)} %broadcast_multiply_fusion, f32[2560]{0:T(1024)S(1)} %convert_element_type.22, f32[2048]{0:T(1024)S(1)} %add_rsqrt_fusion, bf16[1,2048,2560]{2,1,0:T(8,128)(2,1)} %param.10, ...), kind=kLoop, calls=%fused_computation.15 | loop fusion | flops 57671680 | bytes 83912704 | tf_op jit(solution)/shard_map/broadcast_in_dim | solution.py:202
  (4 shorter events, 0.0 us)
Async XLA Ops:
  7.2 287.4 %all-reduce.3.cloned.1.call-start = ((), (), s32[]{:S(2)}) async-start(), calls=%async_computation | async-start | bytes 41943040 | tf_op jit(solution)/shard_map/psum | solution.py:182
  32.5 1.2 copy-start
  33.7 1.0 copy-start.1
  34.8 1.0 copy-start.2
  55.2 475.7 %all-reduce.5.cloned.1.call-start = ((), (), s32[]{:S(2)}) async-start(), calls=%async_computation.1 | async-start | bytes 41943040 | tf_op jit(solution)/shard_map/psum | solution.py:191
  55.7 34.4 %copy-start.3 = (bf16[2560,256]{1,0:T(8,128)(2,1)S(1)}, bf16[2560,256]{1,0:T(8,128)(2,1)}, u32[]{:S(2)}) copy-start(bf16[2560,256]{1,0:T(8,128)(2,1)} %param.12) | copy-start | bytes 3932164
  78.5 8.9 %collective-permute-start = (f32[2048,256]{1,0:T(8,128)}, f32[2048,256]{1,0:T(8,128)S(1)}, u32[]{:S(2)}, u32[]{:S(2)}) collective-permute-start(f32[2048,256]{1,0:T(8,128)} %get-tuple-element.20), channel_id=1, source_target_pairs={{0,1},{1,0},{2,3},{3,2},{4,5},{5,4},{6,7},{7,6},{8,9},{9,8},{10,11... | collective-permute-start | bytes 6291464 | tf_op jit(solution)/shard_map/ppermute | solution.py:160
  101.6 193.1 %copy-start.4 = (bf16[2560]{0:T(1024)(128)(2,1)S(1)}, bf16[2560]{0:T(1024)(128)(2,1)}, u32[]{:S(2)}) copy-start(bf16[2560]{0:T(1024)(128)(2,1)} %param.11) | copy-start | bytes 15364
  294.7 14.8 %slice-start = ((s8[10485760]{0:T(1024)(128)(4,1)}), s8[2097152]{0:T(1024)(128)(4,1)S(1)}, s32[]{:S(2)}) async-start(s8[10485760]{0:T(1024)(128)(4,1)} %bitcast.23), calls=%async_computation.2 | async-start | bytes 4194304
  294.7 14.8 %slice-start.1 = ((s8[10485760]{0:T(1024)(128)(4,1)}), s8[4194304]{0:T(1024)(128)(4,1)S(1)}, s32[]{:S(2)}) async-start(s8[10485760]{0:T(1024)(128)(4,1)} %bitcast.23), calls=%async_computation.3 | async-start | bytes 8388608
  300.9 8.6 %copy-start.5 = (bf16[2048,256]{1,0:T(8,128)(2,1)S(1)}, bf16[2048,256]{1,0:T(8,128)(2,1)}, u32[]{:S(2)}) copy-start(bf16[2048,256]{1,0:T(8,128)(2,1)} %get-tuple-element.19) | copy-start | bytes 3145732
  301.0 8.6 %slice-start.2 = ((s8[10485760]{0:T(1024)(128)(4,1)}), s8[4194304]{0:T(1024)(128)(4,1)S(1)}, s32[]{:S(2)}) async-start(s8[10485760]{0:T(1024)(128)(4,1)} %bitcast.23), calls=%async_computation.4 | async-start | bytes 8388608
Sparse Core Ops, SparseCore 0:
  55.3 239.2 all-reduce.2
  297.0 233.8 all-reduce.4

commit v2 on v1

v2 whole, which is shorter than its diff:
```python
import functools
import math
import jax
import jax.numpy as jnp
import numpy as np
from jax import lax
from jax.experimental import pallas as pl
from jax.experimental.pallas import tpu as pltpu
from jax.sharding import PartitionSpec as P

HEAD_DIM = 128
NORM_EPS = 1.0e-5
ROPE_BASE = 10000.0
MASK_VALUE = -1.0e30
SCORE_SCALE = 1.0 / math.sqrt(HEAD_DIM)
EXP2_SCALE = SCORE_SCALE * math.log2(math.e)
ROWS = 256
BF16 = jnp.bfloat16
F32 = jnp.float32
VMEM_LIMIT = 66 * 10**6


def dot(a, b, contract):
    return lax.dot_general(a, b, ((contract[:1], contract[1:]), ((), ())), preferred_element_type=F32)


def rope_tables(seq_len):
    inv_freq = ROPE_BASE ** (-np.arange(0, HEAD_DIM, 2, dtype=np.float64) / HEAD_DIM)
    angles = np.arange(seq_len, dtype=np.float64)[:, None] * inv_freq[None, :]
    cos_t = np.repeat(np.cos(angles), 2, axis=1)
    sin_t = np.stack([-np.sin(angles), np.sin(angles)], axis=-1).reshape(seq_len, HEAD_DIM)
    return cos_t.astype(np.float32), sin_t.astype(np.float32)


def rotate(t, cos_t, sin_t):
    even = lax.broadcasted_iota(jnp.int32, t.shape, 1) % 2 == 0
    swapped = jnp.where(even, pltpu.roll(t, HEAD_DIM - 1, 1), pltpu.roll(t, 1, 1))
    return t * cos_t + swapped * sin_t


def proj_kernel(x_ref, dout_ref, gain_ref, wqkv_ref, wo_ref, cos_ref, sin_ref, n_ref, q_ref, k_ref, v_ref, do_ref):
    x = x_ref[...].astype(F32)
    inv = lax.rsqrt(jnp.mean(x * x, axis=-1, keepdims=True) + NORM_EPS)
    n = (x * inv * gain_ref[...]).astype(BF16)
    n_ref[...] = n
    qkv = dot(n, wqkv_ref[...], (1, 0))
    cos_t, sin_t = cos_ref[...], sin_ref[...]
    q_ref[:, :HEAD_DIM] = rotate(qkv[:, :HEAD_DIM], cos_t, sin_t).astype(BF16)
    q_ref[:, HEAD_DIM:] = rotate(qkv[:, HEAD_DIM:2 * HEAD_DIM], cos_t, sin_t).astype(BF16)
    k_ref[...] = rotate(qkv[:, 2 * HEAD_DIM:3 * HEAD_DIM], cos_t, sin_t).astype(BF16)
    v_ref[...] = qkv[:, 3 * HEAD_DIM:].astype(BF16)
    do_ref[...] = dot(dout_ref[...], wo_ref[...], (1, 1)).astype(BF16)


def project(x, dout, gain, wqkv, wo, cos_t, sin_t):
    seq, d = x.shape
    row = lambda w: pl.BlockSpec((ROWS, w), lambda i: (i, 0))
    whole = lambda a: pl.BlockSpec(a.shape, lambda i: (0, 0))
    widths = (d, 2 * HEAD_DIM, HEAD_DIM, HEAD_DIM, 2 * HEAD_DIM)
    return pl.pallas_call(
        proj_kernel, grid=(seq // ROWS,),
        in_specs=[row(d), row(d), whole(gain), whole(wqkv), whole(wo), row(HEAD_DIM), row(HEAD_DIM)],
        out_specs=[row(w) for w in widths],
        out_shape=[jax.ShapeDtypeStruct((seq, w), BF16) for w in widths],
        cost_estimate=pl.CostEstimate(flops=2 * seq * d * 6 * HEAD_DIM, bytes_accessed=6 * seq * d, transcendentals=0),
        name='project')(x, dout, gain, wqkv, wo, cos_t, sin_t)


def stack_heads(ref, rows):
    return jnp.concatenate([ref[rows, :HEAD_DIM], ref[rows, HEAD_DIM:]], axis=0)


def attn_fwd_kernel(q_ref, k_ref, v_ref, o_ref, o32_ref):
    seq = q_ref.shape[0]
    row_id = lax.broadcasted_iota(jnp.int32, (2 * ROWS, ROWS), 0) % ROWS
    causal = row_id >= lax.broadcasted_iota(jnp.int32, (2 * ROWS, ROWS), 1)
    for i in range(seq // ROWS):
        lo = i * ROWS
        rows = pl.ds(lo, ROWS)
        q2 = stack_heads(q_ref, rows)
        s_diag = jnp.where(causal, dot(q2, k_ref[rows, :], (1, 1)), MASK_VALUE)
        m = jnp.max(s_diag, axis=-1, keepdims=True)
        if lo:
            s_pre = dot(q2, k_ref[:lo, :], (1, 1))
            m = jnp.maximum(m, jnp.max(s_pre, axis=-1, keepdims=True))
        p_diag = jnp.exp2((s_diag - m) * EXP2_SCALE)
        total = jnp.sum(p_diag, axis=-1, keepdims=True)
        if lo:
            p_pre = jnp.exp2((s_pre - m) * EXP2_SCALE)
            total = total + jnp.sum(p_pre, axis=-1, keepdims=True)
        scale = 1.0 / total
        o2 = dot((p_diag * scale).astype(BF16), v_ref[rows, :], (1, 0))
        if lo:
            o2 = o2 + dot((p_pre * scale).astype(BF16), v_ref[:lo, :], (1, 0))
        o2 = o2.astype(BF16)
        for head in range(2):
            cols = slice(head * HEAD_DIM, (head + 1) * HEAD_DIM)
            o_ref[rows, cols] = o2[head * ROWS:(head + 1) * ROWS]
            o32_ref[rows, cols] = o2[head * ROWS:(head + 1) * ROWS].astype(F32)


def attn_fwd(q, k, v):
    seq = q.shape[0]
    return pl.pallas_call(
        attn_fwd_kernel,
        out_shape=[jax.ShapeDtypeStruct(q.shape, BF16), jax.ShapeDtypeStruct(q.shape, F32)],
        compiler_params=pltpu.CompilerParams(vmem_limit_bytes=48 * 2**20),
        cost_estimate=pl.CostEstimate(flops=4 * seq * seq * HEAD_DIM, bytes_accessed=8 * seq * HEAD_DIM, transcendentals=seq * seq),
        name='attn_fwd')(q, k, v)


def attn_bwd_rows(i, head, q_ref, k_ref, v_ref, do_ref, cos_ref, sin_ref, dq_ref, dq32_ref, dk_acc, dv_acc):
    lo, hi = i * ROWS, (i + 1) * ROWS
    rows, cols = pl.ds(lo, ROWS), pl.ds(head * HEAD_DIM, HEAD_DIM)
    q, do = q_ref[rows, cols], do_ref[rows, cols]
    k_all, v_all = k_ref[:hi, :], v_ref[:hi, :]
    causal = lax.broadcasted_iota(jnp.int32, (ROWS, ROWS), 0) <= lax.broadcasted_iota(jnp.int32, (ROWS, ROWS), 1)
    s_t = dot(k_all, q, (1, 1))
    s_diag = jnp.where(causal, s_t[lo:], MASK_VALUE)
    s_t = jnp.concatenate([s_t[:lo], s_diag], axis=0) if lo else s_diag
    m = jnp.max(s_t, axis=0, keepdims=True)
    p = jnp.exp2((s_t - m) * EXP2_SCALE)
    p = p * (1.0 / jnp.sum(p, axis=0, keepdims=True))
    dp = dot(v_all, do, (1, 1))
    delta = jnp.sum(p * dp, axis=0, keepdims=True)
    ds = (p * (dp - delta) * SCORE_SCALE).astype(BF16)
    dv = dot(p.astype(BF16), do, (1, 0))
    dk = dot(ds, q, (1, 0))
    dq = dot(ds, k_all, (0, 0))
    if head == 0:
        dk_acc[lo:hi, :] = dk[lo:]
        dv_acc[lo:hi, :] = dv[lo:]
        if lo:
            dk_acc[:lo, :] += dk[:lo]
            dv_acc[:lo, :] += dv[:lo]
    else:
        dk_acc[:hi, :] += dk
        dv_acc[:hi, :] += dv
    dq = rotate(dq, cos_ref[rows, :], -sin_ref[rows, :]).astype(BF16)
    dq_ref[rows, cols] = dq
    dq32_ref[rows, cols] = dq.astype(F32)


SUBS = 2


def ring_kernel_setup(n):
    me = lax.axis_index('tp')
    chip, core = me // 2, me % 2
    right = (chip + 1) % n * 2 + core
    left = (chip + n - 1) % n * 2 + core
    sib = me + 1 - 2 * core
    barrier = pltpu.get_barrier_semaphore()
    for peer in (right, left, sib):
        pl.semaphore_signal(barrier, inc=1, device_id={'tp': peer}, device_id_type=pl.DeviceIdType.MESH)
    pl.semaphore_wait(barrier, 3)
    return chip, core, right, left, sib


def remote(src, dst, send, recv, peer):
    return pltpu.make_async_remote_copy(src_ref=src, dst_ref=dst, send_sem=send, recv_sem=recv,
                                        device_id={'tp': peer}, device_id_type=pl.DeviceIdType.MESH)


def ring_sum(n, place, extra, partial, finish, rider, out_ref, gain_acc, bufs, sems):
    chip, core, right, left, sib = place
    rs_buf, ag_buf, sib_buf, obuf = bufs
    rs_send, rs_recv, ag_send, ag_recv, sib_send, sib_recv, out_sem, credit = sems
    width = rs_buf.shape[-1]
    block = out_ref.shape[0] // n
    sub_rows = block // SUBS
    half = 2 * width
    peers = (right, left)

    def part(slot_ref, sub, with_extra):
        return slot_ref.at[pl.ds(sub * sub_rows, sub_rows + (extra if with_extra and sub == SUBS - 1 else 0)), :]

    def rs_copy(s, sub, way):
        return remote(part(rs_buf.at[way, s], sub, False), part(rs_buf.at[way, s + 1], sub, False),
                      rs_send.at[way, s, sub], rs_recv.at[way, s, sub], peers[way])

    def ag_copy(s, sub, way):
        return remote(part(ag_buf.at[way, s], sub, True), part(ag_buf.at[way, s + 1], sub, True),
                      ag_send.at[way, s, sub], ag_recv.at[way, s, sub], peers[way])

    def sib_copy(s, sub, way):
        rows = sub_rows + (extra if sub == SUBS - 1 else 0)
        k = SUBS * s + sub
        return remote(part(ag_buf.at[way, s], sub, True), sib_buf.at[way, k % 4, pl.ds(0, rows), :],
                      sib_send.at[way, k], sib_recv.at[way, k], sib)

    def my_part(dest, sub, way):
        row = pl.multiple_of(dest * block + sub * sub_rows, sub_rows)
        return partial(pl.ds(row, sub_rows), way)

    def dest_of(s, way):
        return (chip + n - 1 - s) % n if way == 0 else (chip + 1 + s) % n

    def local(ref, sub):
        return pl.ds(sub * sub_rows, sub_rows)

    for sub in range(SUBS):
        for way in range(2):
            rs_buf[way, 0, local(rs_buf, sub), :] = my_part(dest_of(0, way), sub, way)
            rs_copy(0, sub, way).start()
    rider(0)

    def rs_step(s, carry):
        for sub in range(SUBS):
            for way in range(2):
                rs_copy(s - 1, sub, way).wait_recv()
                rs_buf[way, s, local(rs_buf, sub), :] += my_part(dest_of(s, way), sub, way)
                rs_copy(s, sub, way).start()
            if sub == 0:
                rider(s)
        return carry

    lax.fori_loop(1, n - 1, rs_step, 0)
    for sub in range(SUBS):
        for way in range(2):
            rs_copy(n - 2, sub, way).wait_recv()
        finish(sub, [rs_buf[way, n - 1, local(rs_buf, sub), :] + my_part(chip, sub, way) for way in range(2)])

    def out_copy(whose, s, sub, way):
        b = (chip + n - s) % n if way == 0 else (chip + s) % n
        col = (core if whose == 0 else 1 - core) * half + way * width
        dst = out_ref.at[pl.ds(pl.multiple_of(b * block + sub * sub_rows, sub_rows), sub_rows), pl.ds(pl.multiple_of(col, 128), width)]
        return pltpu.make_async_copy(obuf.at[whose, sub, way], dst, out_sem.at[whose, sub, way])

    def emit(whose, s, sub, way, values):
        @pl.when(s >= 1)
        def _():
            out_copy(whose, s - 1, sub, way).wait()
        obuf[whose, sub, way] = values.astype(BF16)
        out_copy(whose, s, sub, way).start()

    def own_chunk(s, sub, forward):
        @pl.when(s >= 2)
        def _():
            pl.semaphore_wait(credit, 1)
        for way in range(2):
            if forward:
                ag_copy(s, sub, way).start()
            sib_copy(s, sub, way).start()
        for way in range(2):
            emit(0, s, sub, way, ag_buf[way, s, local(ag_buf, sub), :])
            if extra and sub == SUBS - 1:
                gain_acc[0, way] += ag_buf[way, s, pl.ds(block, extra), :]

    def sib_chunk(s, sub):
        k = SUBS * s + sub
        for way in range(2):
            sib_copy(s, sub, way).wait_recv()
            emit(1, s, sub, way, sib_buf[way, k % 4, pl.ds(0, sub_rows), :])
            if extra and sub == SUBS - 1:
                gain_acc[1, way] += sib_buf[way, k % 4, pl.ds(sub_rows, extra), :]

        @pl.when(s < n - 2)
        def _():
            pl.semaphore_signal(credit, inc=1, device_id={'tp': sib}, device_id_type=pl.DeviceIdType.MESH)

    own_chunk(0, 0, True)
    own_chunk(0, 1, True)
    rider(n - 1)
    sib_chunk(0, 0)

    def ag_step(s, carry):
        for sub in range(SUBS):
            for way in range(2):
                ag_copy(s - 1, sub, way).wait_recv()
            own_chunk(s, sub, True)
            if sub == 0:
                sib_chunk(s - 1, 1)
            else:
                sib_chunk(s, 0)
        return carry

    lax.fori_loop(1, n - 1, ag_step, 0)
    last = n - 1
    for sub in range(SUBS):
        for way in range(2):
            ag_copy(last - 1, sub, way).wait_recv()
        own_chunk(last, sub, False)
        if sub == 0:
            sib_chunk(last - 1, 1)
        else:
            sib_chunk(last, 0)
    sib_chunk(last, 1)
    for sub in range(SUBS):
        for way in range(2):
            for whose in range(2):
                out_copy(whose, last, sub, way).wait()

    def drain(s, carry):
        for sub in range(SUBS):
            for way in range(2):
                rs_copy(s, sub, way).wait_send()
                ag_copy(s, sub, way).wait_send()
                sib_copy(s, sub, way).wait_send()
        return carry

    lax.fori_loop(0, n - 1, drain, 0)
    for sub in range(SUBS):
        for way in range(2):
            sib_copy(last, sub, way).wait_send()


def ring_scratch(n, seq, d_model, extra):
    width, block = d_model // 4, seq // n
    sub_rows = block // SUBS
    dma = pltpu.SemaphoreType.DMA
    return [
        pltpu.VMEM((2, n, block, width), F32),
        pltpu.VMEM((2, n, block + extra, width), F32),
        pltpu.VMEM((2, 4, sub_rows + extra, width), F32),
        pltpu.VMEM((2, SUBS, 2, sub_rows, width), BF16),
        dma((2, n - 1, SUBS)), dma((2, n - 1, SUBS)), dma((2, n - 1, SUBS)), dma((2, n - 1, SUBS)),
        dma((2, SUBS * n)), dma((2, SUBS * n)), dma((2, SUBS, 2)), pltpu.SemaphoreType.REGULAR,
    ]


def out_kernel(n, riders, o_ref, osib_ref, wo_ref, wosib_ref, x_ref, q_ref, k_ref, v_ref, do_ref, cos_ref, sin_ref,
               out_ref, dq_ref, dq32_ref, dkv_ref, lhs, rhs, x_rows, dk_acc, row_sem, *ring):
    bufs, sems = ring[:4], ring[4:]
    place = ring_kernel_setup(n)
    chip, core = place[:2]
    width = bufs[0].shape[-1]
    block = x_rows.shape[0]
    inner = o_ref.shape[1]
    x_copy = pltpu.make_async_copy(
        x_ref.at[pl.ds(pl.multiple_of(chip * block, block), block), pl.ds(pl.multiple_of(core * 2 * width, 128), 2 * width)],
        x_rows, row_sem)
    x_copy.start()
    lhs[:, :inner] = o_ref[...]
    lhs[:, inner:] = osib_ref[...].astype(BF16)
    rhs[:inner, :] = wo_ref[...]
    rhs[inner:, :] = wosib_ref[...].astype(BF16)

    def partial(rows, way):
        return dot(lhs[rows, :], rhs[:, way * width:(way + 1) * width], (1, 0))

    sub_rows = block // SUBS

    def finish(sub, sums):
        if sub == 0:
            x_copy.wait()
        for way in range(2):
            rows = pl.ds(sub * sub_rows, sub_rows)
            bufs[1][way, 0, rows, :] = sums[way] + x_rows[rows, way * width:(way + 1) * width].astype(F32)

    dv_acc = dkv_ref.at[:, pl.ds(HEAD_DIM, HEAD_DIM)]
    count = q_ref.shape[0] // ROWS

    def ride(step):
        for i in range(step * count // n, (step + 1) * count // n):
            for head in range(2):
                attn_bwd_rows(i, head, q_ref, k_ref, v_ref, do_ref, cos_ref, sin_ref, dq_ref, dq32_ref, dk_acc, dv_acc)
        if step == n - 1:
            dkv_ref[:, :HEAD_DIM] = rotate(dk_acc[...], cos_ref[...], -sin_ref[...])

    def rider(step):
        if not riders:
            return
        if isinstance(step, int):
            ride(step)
        else:
            for static in range(1, n - 1):
                pl.when(step == static)(lambda static=static: ride(static))

    ring_sum(n, place, 0, partial, finish, rider, out_ref, None, bufs, sems)


def grad_kernel(n, dq_ref, dqsib_ref, dkv_ref, dkvsib_ref, wq_ref, wqsib_ref, wkv_ref, x_ref, dout_ref, gain_ref,
                out_ref, gsum_ref, lhs, rhs, x_rows, dout_rows, unit_buf, stat_buf, gain_acc, row_sem, stat_send, stat_recv, *ring):
    bufs, sems = ring[:4], ring[4:]
    place = ring_kernel_setup(n)
    chip, core, right, left, sib = place
    width = bufs[0].shape[-1]
    block = x_rows.shape[0]
    inner = dq_ref.shape[1]
    half = 2 * width
    row = pl.multiple_of(chip * block, block)
    col = pl.multiple_of(core * half, 128)
    x_copy = pltpu.make_async_copy(x_ref.at[pl.ds(row, block), :], x_rows, row_sem.at[0])
    dout_copy = pltpu.make_async_copy(dout_ref.at[pl.ds(row, block), pl.ds(col, half)], dout_rows, row_sem.at[1])
    x_copy.start()
    dout_copy.start()
    lhs[:, :inner] = dq_ref[...]
    lhs[:, inner:2 * inner] = dqsib_ref[...].astype(BF16)
    lhs[:, 2 * inner:] = (dkv_ref[...] + dkvsib_ref[...]).astype(BF16)
    rhs[:, :inner] = wq_ref[...]
    rhs[:, inner:2 * inner] = wqsib_ref[...].astype(BF16)
    rhs[:, 2 * inner:] = wkv_ref[...]
    gain_acc[...] = jnp.zeros_like(gain_acc)

    def partial(rows, way):
        return dot(lhs[rows, :], rhs[way * width:(way + 1) * width, :], (1, 1))

    sub_rows = block // SUBS

    def prepare(sub):
        rows = pl.ds(sub * sub_rows, sub_rows)
        x = x_rows[rows, :].astype(F32)
        inv = lax.rsqrt(jnp.mean(x * x, axis=-1, keepdims=True) + NORM_EPS)
        stat_buf[2, rows, :] = jnp.broadcast_to(inv, (sub_rows, HEAD_DIM))
        mine = x_rows[rows, pl.ds(col, half)].astype(F32)
        unit_buf[rows, :] = mine * inv

    def rider(step):
        if isinstance(step, int) and step == 0:
            x_copy.wait()
            dout_copy.wait()
            for sub in range(SUBS):
                prepare(sub)

    def stat_copy(sub):
        rows = pl.ds(sub * sub_rows, sub_rows)
        return remote(stat_buf.at[0, rows, :], stat_buf.at[1, rows, :], stat_send.at[sub], stat_recv.at[sub], sib)

    def finish(sub, sums):
        rows = pl.ds(sub * sub_rows, sub_rows)
        ag_buf = bufs[1]
        total = jnp.zeros((sub_rows, 1), F32)
        for way in range(2):
            cols = slice(way * width, (way + 1) * width)
            unit = unit_buf[rows, cols]
            prod = sums[way] * unit
            total = total + jnp.sum(prod * gain_ref[:, cols], axis=-1, keepdims=True)
            gsum = jnp.sum(prod.reshape(sub_rows // 8, 8, width), axis=0)
            ag_buf[way, 0, pl.ds(block, 8), :] = gsum if sub == 0 else gsum + ag_buf[way, 0, pl.ds(block, 8), :]
            ag_buf[way, 0, rows, :] = sums[way]
        stat_buf[0, rows, :] = jnp.broadcast_to(total, (sub_rows, HEAD_DIM))
        stat_copy(sub).start()
        stat_copy(sub).wait()
        mean = (stat_buf[0, rows, 0:1] + stat_buf[1, rows, 0:1]) * (1.0 / (2 * half))
        inv = stat_buf[2, rows, 0:1]
        for way in range(2):
            cols = slice(way * width, (way + 1) * width)
            scaled = ag_buf[way, 0, rows, :] * gain_ref[:, cols]
            ag_buf[way, 0, rows, :] = dout_rows[rows, cols].astype(F32) + inv * (scaled - unit_buf[rows, cols] * mean)

    ring_sum(n, place, 8, partial, finish, rider, out_ref, gain_acc, bufs, sems)
    for way in range(2):
        gsum_ref[core, way] = jnp.sum(gain_acc[0, way], axis=0, keepdims=True)
        gsum_ref[1 - core, way] = jnp.sum(gain_acc[1, way], axis=0, keepdims=True)


def out_sum(n, o, o_sib, wo, wo_sib, x, q, k, v, do, cos_t, sin_t):
    seq, d_model = x.shape
    half = d_model // 2
    vmem, hbm = pl.BlockSpec(memory_space=pltpu.VMEM), pl.BlockSpec(memory_space=pl.ANY)
    shape = jax.ShapeDtypeStruct
    return pl.pallas_call(
        functools.partial(out_kernel, n, True),
        out_shape=[shape((seq, d_model), BF16), shape(q.shape, BF16), shape(q.shape, F32), shape((seq, 2 * HEAD_DIM), F32)],
        in_specs=[vmem] * 4 + [hbm] + [vmem] * 6, out_specs=[hbm] + [vmem] * 3,
        scratch_shapes=[pltpu.VMEM((seq, 2 * o.shape[1]), BF16), pltpu.VMEM((2 * o.shape[1], half), BF16),
                        pltpu.VMEM((seq // n, half), BF16), pltpu.VMEM((seq, HEAD_DIM), F32), pltpu.SemaphoreType.DMA]
        + ring_scratch(n, seq, d_model, 0),
        compiler_params=pltpu.CompilerParams(collective_id=1, has_side_effects=True, vmem_limit_bytes=VMEM_LIMIT),
        cost_estimate=pl.CostEstimate(flops=10 * seq * seq * HEAD_DIM, bytes_accessed=4 * seq * d_model, transcendentals=seq * seq),
        name='out_sum')(o, o_sib, wo, wo_sib, x, q, k, v, do, cos_t, sin_t)


def grad_sum(n, dq, dq_sib, dkv, dkv_sib, wq, wq_sib, wkv, x, dout, gain):
    seq, d_model = x.shape
    half, block, width = d_model // 2, seq // n, d_model // 4
    kdim = 2 * dq.shape[1] + dkv.shape[1]
    vmem, hbm = pl.BlockSpec(memory_space=pltpu.VMEM), pl.BlockSpec(memory_space=pl.ANY)
    shape = jax.ShapeDtypeStruct
    dma = pltpu.SemaphoreType.DMA
    return pl.pallas_call(
        functools.partial(grad_kernel, n),
        out_shape=[shape((seq, d_model), BF16), shape((2, 2, 1, width), F32)],
        in_specs=[vmem] * 7 + [hbm] * 2 + [vmem], out_specs=[hbm, vmem],
        scratch_shapes=[pltpu.VMEM((seq, kdim), BF16), pltpu.VMEM((half, kdim), BF16),
                        pltpu.VMEM((block, d_model), BF16), pltpu.VMEM((block, half), BF16), pltpu.VMEM((block, half), F32),
                        pltpu.VMEM((3, block, HEAD_DIM), F32), pltpu.VMEM((2, 2, 8, width), F32),
                        dma((2,)), dma((SUBS,)), dma((SUBS,))]
        + ring_scratch(n, seq, d_model, 8),
        compiler_params=pltpu.CompilerParams(collective_id=2, has_side_effects=True, vmem_limit_bytes=VMEM_LIMIT),
        cost_estimate=pl.CostEstimate(flops=4 * seq * kdim * half, bytes_accessed=4 * seq * d_model, transcendentals=0),
        name='grad_sum')(dq, dq_sib, dkv, dkv_sib, wq, wq_sib, wkv, x, dout, gain)


def solution(mesh):
    tp_size = mesh.shape['tp']
    chips = tp_size // 2
    swap = [(source, source ^ 1) for source in range(tp_size)]

    def block_fn(hidden, grad_out, norm_gain, w_query, w_key, w_value, w_out):
        batch, seq_len, d_model = hidden.shape
        half = d_model // 2
        tp_index = lax.axis_index('tp')
        kv_index, core = tp_index // 2, tp_index % 2
        w_k = lax.dynamic_slice_in_dim(w_key, kv_index * HEAD_DIM, HEAD_DIM, axis=1)
        w_v = lax.dynamic_slice_in_dim(w_value, kv_index * HEAD_DIM, HEAD_DIM, axis=1)
        w_qkv = jnp.concatenate([w_query, w_k, w_v], axis=1)
        cos_t, sin_t = rope_tables(seq_len)
        x, dout = hidden[0], grad_out[0]
        gain = norm_gain.astype(F32)[None, :]
        mine, other = core * half, (1 - core) * half
        wo_mine = lax.dynamic_slice_in_dim(w_out, mine, half, axis=1)
        wo_sib = lax.ppermute(lax.dynamic_slice_in_dim(w_out, other, half, axis=1).astype(F32), 'tp', swap)
        wqkv_mine = lax.dynamic_slice_in_dim(w_qkv, mine, half, axis=0)
        wq_sib = lax.ppermute(lax.dynamic_slice_in_dim(w_query, other, half, axis=0).astype(F32), 'tp', swap)

        n, q, k, v, do = project(x, dout, gain, w_qkv, w_out, cos_t, sin_t)
        o, o32 = attn_fwd(q, k, v)
        o_sib = lax.ppermute(o32, 'tp', swap)
        block_out, dq, dq32, dkv32 = out_sum(chips, o, o_sib, wo_mine, wo_sib, x, q, k, v, do, cos_t, sin_t)
        dq_sib = lax.ppermute(dq32, 'tp', swap)
        dkv_sib = lax.ppermute(dkv32, 'tp', swap)
        gain_mine = lax.dynamic_slice_in_dim(gain, mine, half, axis=1)
        inner = w_query.shape[1]
        grad_hidden, gain_sum = grad_sum(chips, dq, dq_sib, dkv32, dkv_sib, wqkv_mine[:, :inner], wq_sib, wqkv_mine[:, inner:],
                                         x, dout, gain_mine)
        dkv = (dkv32 + dkv_sib).astype(BF16)
        grad_w_out = dot(o, dout, (0, 0))
        grad_w_query = dot(n, dq, (0, 0))
        grad_w_key = dot(n, dkv[:, :HEAD_DIM], (0, 0))
        grad_w_value = dot(n, dkv[:, HEAD_DIM:], (0, 0))
        return block_out[None], grad_hidden[None], gain_sum.reshape(-1), grad_w_query, grad_w_key, grad_w_value, grad_w_out

    act_spec = P('dp', None, None)
    return jax.shard_map(
        block_fn, mesh=mesh,
        in_specs=(act_spec, act_spec, P(None), P(None, 'tp'), P(None, None), P(None, None), P('tp', None)),
        out_specs=(act_spec, act_spec, P('dp'), P('dp', 'tp'), P('dp', 'tp'), P('dp', 'tp'), P(('dp', 'tp'), None)),
        check_vma=False)
```

time: 589 us -> 543 us (0.922)
  Pallas kernels: 51.7 us -> 464 us
  waiting for transfers between devices: 406 us -> 0.01 us
  other arithmetic: 53.6 us -> 6.76 us
  local copies, waits for them, and re-layouts: 6.04 us -> 29.2 us
  matrix products: 42.5 us -> 25.4 us
  between operations: 14.7 us -> 1.23 us
    pallas_call x2 -> x3, Pallas kernels: 32.2 us -> 444 us  [the longest x1 218 us: grad_sum(): pl.pallas_call(functools.partial(grad_kernel, n), out_shape=[shape((seq,...]
    psum x2 -> x0, waiting for transfers between devices: 402 us -> none  [the longest x1 209 us: block_fn(): dn = lax.psum(dn_part, 'tp')]
    broadcast_in_dim x1 -> x0, other arithmetic: 28.7 us -> none  [block_fn(): grad_hidden[None]]
    unnamed x18 -> x28, local copies, waits for them, and re-layouts: 3.34 us -> 22.8 us
    reduce_sum x2 -> x0, other arithmetic: 19.2 us -> none  [the longest x1 13 us: block_fn(): grad_gain = jnp.sum(dn * unit, axis=0)]
    dot_general x6 -> x4, matrix products: 42.5 us -> 25.4 us  [dot(): lax.dot_general(a, b, ((contract[:1], contract[1:]), ((), ())), preferred...]
  transfers between devices with their start and end apart: 3 -> 5, of which waited for: 3 -> 0; matrix products, arithmetic and copies ran while one was open for 7% -> 6% of each run, Pallas kernels for 4% -> 41%
where the time goes in v2:
time: 543 us; the launch traced here: 532 us
  Pallas kernels  464 us (85%)
  local copies, waits for them, and re-layouts  29.2 us (5%)
  matrix products  25.4 us (5%)
  other arithmetic  6.76 us (1%)
  starting transfers between devices  5.95 us (1%)
    pallas_call x1, Pallas kernels, grad_sum(): pl.pallas_call(functools.partial(grad_kernel, n), out_shape=[shape((seq,...  218 us
    pallas_call x1, Pallas kernels, out_sum(): pl.pallas_call(functools.partial(out_kernel, n, True), out_shape=[shape((...  217 us
    dot_general x4, matrix products, dot(): lax.dot_general(a, b, ((contract[:1], contract[1:]), ((), ())), preferred...  25.4 us
    unnamed x28, local copies, waits for them, and re-layouts  22.8 us
    pallas_call x1, Pallas kernels, project(): pl.pallas_call(proj_kernel, grid=(seq // ROWS,), in_specs=[row(d), row(d)...  19.5 us
  transfers between devices with their start and end apart: 5, of which 0 were waited for; matrix products, arithmetic and copies ran while one was open for 6% of the time, Pallas kernels for 41%

profile of v2, /device:TPU:21, one launch (start us, length us, event | category | flops | bytes accessed | tf_op | source)
XLA Modules:
  0.0 532.5 jit_solution(6240458439009468842)
XLA Ops:
  0.6 0.0 copy-start.6
  0.7 1.4 broadcast_in_dim.9.gain_ref
  2.1 1.4 constant_dynamic-slice_fusion.2
  3.4 0.0 copy-done.6
  3.5 1.7 pad_maximum_fusion.wqkv_ref
  5.2 19.5 %project.1 = (bf16[2048,2560]{1,0:T(8,128)(2,1)}, bf16[2048,256]{1,0:T(8,128)(2,1)}, bf16[2048,128]{1,0:T(8,128)(2,1)}, bf16[2048,128]{1,0:T(8,128)(2,1)}, bf16[2048,256]{1,0:T(8,128)(2,1)}) custom-call(bf16[2048,2560]{1,0:T(8,128)(2,1)} %bitcast.13, bf16[2048,2560]{1,0:T(8,128)(2,1)} %bitcast.11, f32[1,2560]{1,0:T(1,128)} %broadcast_in_dim.9.gain_ref, ...), custom_call_target="tpu_custom_call" | custom-call | flops 8053063680 | bytes 31457280 | tf_op jit(solution)/shard_map/project/pallas_call | solution.py:60
  24.7 0.0 copy-start.1
  24.7 1.2 copy-done.1
  25.9 0.0 copy-start.2
  25.9 1.0 copy-done.2
  27.0 0.0 copy-start.3
  27.0 1.0 copy-done.3
  28.0 9.5 %attn_fwd.1 = (bf16[2048,256]{1,0:T(8,128)(2,1)S(1)}, f32[2048,256]{1,0:T(8,128)S(1)}) custom-call(bf16[2048,256]{1,0:T(8,128)(2,1)S(1)} %copy-done.1, bf16[2048,128]{1,0:T(8,128)(2,1)S(1)} %copy-done.2, bf16[2048,128]{1,0:T(8,128)(2,1)S(1)} %copy-done.3), custom_call_target="tpu_custom_call" | custom-call | flops 2147483648 | bytes 2097152 | tf_op jit(solution)/shard_map/attn_fwd/pallas_call | solution.py:104
  37.5 0.0 copy-start
  37.5 1.0 copy-done
  38.5 4.7 collective-permute-start
  43.1 0.0 copy-start.8
  43.1 2.8 dynamic-slice_convert_fusion.1
  45.9 0.0 collective-permute-start.1
  45.9 1.2 dynamic-slice_convert_fusion
  47.1 0.5 collective-permute-start.4
  47.6 0.0 copy-done.8
  47.6 0.1 dynamic-slice.3
  47.7 0.6 dynamic_slice.27.gain_ref
  48.3 2.4 fusion.6
  50.7 0.0 collective-permute-done.1.wosib_ref
  50.7 0.0 collective-permute-done.osib_ref
  50.7 217.1 %out_sum.1 = (bf16[2048,2560]{1,0:T(8,128)(2,1)}, bf16[2048,256]{1,0:T(8,128)(2,1)}, f32[2048,256]{1,0:T(8,128)}, f32[2048,256]{1,0:T(8,128)}) custom-call(bf16[2048,256]{1,0:T(8,128)(2,1)} %copy-done, f32[2048,256]{1,0:T(8,128)} %collective-permute-done.osib_ref, bf16[256,1280]{1,0:T(8,128)(2,1)} %get-tuple-element.36.wo_ref, ...), custom_call_target="tpu_custom_call" | custom-call | flops 5368709120 | bytes 20971520 | tf_op jit(solution)/shard_map/out_sum/pallas_call | solution.py:453
  267.8 0.0 copy-start.9
  267.8 0.0 copy-start.7
  267.8 0.1 collective-permute-start.3
  267.9 0.0 slice-start
  267.9 0.0 slice-start.1
  267.9 8.8 %fusion.4 = f32[256,2560]{1,0:T(8,128)} fusion(bf16[2048,256]{1,0:T(8,128)(2,1)} %copy-done, bf16[1,2048,2560]{2,1,0:T(8,128)(2,1)} %param.10), kind=kOutput, calls=%fused_computation.12 | convolution fusion | flops 2684354560 | bytes 14155776 | tf_op jit(solution)/shard_map/dot_general | solution.py:24
  276.8 0.0 copy-done.9
  276.8 0.7 collective-permute-start.2
  277.5 0.0 copy-done.7
  277.5 0.0 copy-start.4
  277.5 0.0 slice-start.2
  277.5 8.6 %fusion.7 = f32[2560,256]{1,0:T(8,128)} fusion(bf16[2048,2560]{1,0:T(8,128)(2,1)} %get-tuple-element.32, bf16[2048,256]{1,0:T(8,128)(2,1)S(1)} %copy-done.7), kind=kOutput, calls=%fused_computation.15 | convolution fusion | flops 2684354560 | bytes 14155776 | tf_op jit(solution)/shard_map/dot_general | solution.py:24
  286.0 0.0 collective-permute-done.3.dkvsib_ref
  286.0 0.0 copy-done.4
  286.0 0.0 copy-start.5
  286.0 0.3 add_convert_fusion
  286.4 1.0 copy-done.5
  287.3 0.0 slice-done
  287.3 0.0 slice-done.1
  287.3 0.0 slice-done.2
  287.4 4.0 fusion
  291.3 4.0 fusion.2
  295.3 0.0 collective-permute-done.4.wqsib_ref
  295.3 0.0 collective-permute-done.2.dqsib_ref
  295.3 217.9 %grad_sum.1 = (bf16[2048,2560]{1,0:T(8,128)(2,1)}, f32[2,2,1,640]{3,2,1,0:T(1,128)}) custom-call(bf16[2048,256]{1,0:T(8,128)(2,1)} %get-tuple-element.27.dq_ref, f32[2048,256]{1,0:T(8,128)} %collective-permute-done.2.dqsib_ref, f32[2048,256]{1,0:T(8,128)} %get-tuple-element.29.dkv_ref, f32[2048,256]{1,0:T(8,128)} %copy-done.5, ...), custom_call_target="tpu_custom_call" | custom-call | flops 8053063680 | bytes 20971520 | tf_op jit(solution)/shard_map/grad_sum/pallas_call | solution.py:472
  513.2 0.7 reduce
  514.0 0.6 reshape.18
  514.6 8.7 %copy.18 = bf16[1,2048,2560]{2,1,0:T(8,128)(2,1)} copy(bf16[1,2048,2560]{2,1,0:T(8,128)(2,1)} %bitcast.16) | data formatting | bytes 20971520
  523.3 8.7 %copy.19 = bf16[1,2048,2560]{2,1,0:T(8,128)(2,1)} copy(bf16[1,2048,2560]{2,1,0:T(8,128)(2,1)} %bitcast.17) | data formatting | bytes 20971520
  (1 shorter events, 0.0 us)
Async XLA Ops:
  0.6 2.8 copy-start.6
  24.7 1.2 copy-start.1
  25.9 1.0 copy-start.2
  27.0 1.0 copy-start.3
  37.5 1.0 copy-start
  38.5 12.2 %collective-permute-start = (f32[2048,256]{1,0:T(8,128)S(1)}, f32[2048,256]{1,0:T(8,128)}, u32[]{:S(2)}, u32[]{:S(2)}) collective-permute-start(f32[2048,256]{1,0:T(8,128)S(1)} %get-tuple-element.24), channel_id=1, source_target_pairs={{0,1},{1,0},{2,3},{3,2},{4,5},{5,4},{6,7},{7,6},{8,9},{9,8},{10,11... | collective-permute-start | bytes 6291464 | tf_op jit(solution)/shard_map/ppermute | solution.py:510
  43.1 4.4 copy-start.8
  45.9 4.8 collective-permute-start.1
  47.1 248.3 %collective-permute-start.4 = (f32[1280,256]{1,0:T(8,128)}, f32[1280,256]{1,0:T(8,128)}, u32[]{:S(2)}, u32[]{:S(2)}) collective-permute-start(f32[1280,256]{1,0:T(8,128)} %dynamic-slice_convert_fusion), channel_id=1, source_target_pairs={{0,1},{1,0},{2,3},{3,2},{4,5},{5,4},{6,7},{7,6},{8,9},{9,8},{10,11... | collective-permute-start | bytes 3932168 | tf_op jit(solution)/shard_map/ppermute | solution.py:506
  267.8 9.0 %copy-start.9 = (f32[2048,256]{1,0:T(8,128)S(1)}, f32[2048,256]{1,0:T(8,128)}, u32[]{:S(2)}) copy-start(f32[2048,256]{1,0:T(8,128)} %get-tuple-element.28) | copy-start | bytes 6291460
  267.8 9.7 %copy-start.7 = (bf16[2048,256]{1,0:T(8,128)(2,1)S(1)}, bf16[2048,256]{1,0:T(8,128)(2,1)}, u32[]{:S(2)}) copy-start(bf16[2048,256]{1,0:T(8,128)(2,1)} %get-tuple-element.27.dq_ref) | copy-start | bytes 3145732
  267.8 18.2 %collective-permute-start.3 = (f32[2048,256]{1,0:T(8,128)}, f32[2048,256]{1,0:T(8,128)S(1)}, u32[]{:S(2)}, u32[]{:S(2)}) collective-permute-start(f32[2048,256]{1,0:T(8,128)} %get-tuple-element.29.dkv_ref), channel_id=1, source_target_pairs={{0,1},{1,0},{2,3},{3,2},{4,5},{5,4},{6,7},{7,6},{8,9},{9,8},{10,11... | collective-permute-start | bytes 6291464 | tf_op jit(solution)/shard_map/ppermute | solution.py:513
  267.9 19.4 %slice-start = ((s8[10485760]{0:T(1024)(128)(4,1)}), s8[4194304]{0:T(1024)(128)(4,1)S(1)}, s32[]{:S(2)}) async-start(s8[10485760]{0:T(1024)(128)(4,1)} %bitcast.18), calls=%async_computation | async-start | bytes 8388608
  267.9 19.4 %slice-start.1 = ((s8[10485760]{0:T(1024)(128)(4,1)}), s8[4194304]{0:T(1024)(128)(4,1)S(1)}, s32[]{:S(2)}) async-start(s8[10485760]{0:T(1024)(128)(4,1)} %bitcast.18), calls=%async_computation.1 | async-start | bytes 8388608
  276.8 18.5 %collective-permute-start.2 = (f32[2048,256]{1,0:T(8,128)S(1)}, f32[2048,256]{1,0:T(8,128)}, u32[]{:S(2)}, u32[]{:S(2)}) collective-permute-start(f32[2048,256]{1,0:T(8,128)S(1)} %copy-done.9), channel_id=1, source_target_pairs={{0,1},{1,0},{2,3},{3,2},{4,5},{5,4},{6,7},{7,6},{8,9},{9,8},{10,11... | collective-permute-start | bytes 6291464 | tf_op jit(solution)/shard_map/ppermute | solution.py:512
  277.5 8.6 %copy-start.4 = (f32[2048,256]{1,0:T(8,128)S(1)}, f32[2048,256]{1,0:T(8,128)}, u32[]{:S(2)}) copy-start(f32[2048,256]{1,0:T(8,128)} %get-tuple-element.29.dkv_ref) | copy-start | bytes 6291460
  277.5 9.9 %slice-start.2 = ((s8[10485760]{0:T(1024)(128)(4,1)}), s8[2097152]{0:T(1024)(128)(4,1)S(1)}, s32[]{:S(2)}) async-start(s8[10485760]{0:T(1024)(128)(4,1)} %bitcast.18), calls=%async_computation.2 | async-start | bytes 4194304
  286.0 1.3 copy-start.5

commit v3 on v2

v3 whole, which is shorter than its diff:
```python
import functools
import math
import jax
import jax.numpy as jnp
import numpy as np
from jax import lax
from jax.experimental import pallas as pl
from jax.experimental.pallas import tpu as pltpu
from jax.sharding import PartitionSpec as P

HEAD_DIM = 128
NORM_EPS = 1.0e-5
ROPE_BASE = 10000.0
MASK_VALUE = -1.0e30
SCORE_SCALE = 1.0 / math.sqrt(HEAD_DIM)
EXP2_SCALE = SCORE_SCALE * math.log2(math.e)
ROWS = 256
WIDE = 512
BF16 = jnp.bfloat16
F32 = jnp.float32
VMEM_LIMIT = 66 * 10**6


def dot(a, b, contract):
    return lax.dot_general(a, b, ((contract[:1], contract[1:]), ((), ())), preferred_element_type=F32)


def rope_tables(count):
    def table(positions):
        inv_freq = ROPE_BASE ** (-np.arange(0, HEAD_DIM, 2, dtype=np.float64) / HEAD_DIM)
        angles = positions[:, None] * inv_freq[None, :]
        cos_t = np.repeat(np.cos(angles), 2, axis=1)
        sin_t = np.stack([-np.sin(angles), np.sin(angles)], axis=-1).reshape(cos_t.shape)
        return np.stack([cos_t, sin_t]).astype(np.float32)
    return table(np.arange(ROWS, dtype=np.float64)), table(ROWS * np.arange(count, dtype=np.float64))


def rope_block(b, low_ref, high_ref):
    cos_b, sin_b = high_ref[0, pl.ds(b, 1), :], high_ref[1, pl.ds(b, 1), :]
    cos_l, sin_l = low_ref[0], low_ref[1]
    return cos_b * cos_l - sin_b * sin_l, sin_b * cos_l + cos_b * sin_l


def rotate(t, cos_t, sin_t):
    even = lax.broadcasted_iota(jnp.int32, t.shape, 1) % 2 == 0
    swapped = jnp.where(even, pltpu.roll(t, HEAD_DIM - 1, 1), pltpu.roll(t, 1, 1))
    return t * cos_t + swapped * sin_t


def front_kernel(kv_ref, x_ref, gain_ref, wq_ref, wk_ref, wv_ref, low_ref, high_ref,
                 n_ref, q_ref, k_ref, v_ref, o_ref, wqkv, k_all, v_all):
    i = pl.program_id(0)
    seq = k_all.shape[0]

    @pl.when(i == 0)
    def _():
        k_all[...] = jnp.zeros_like(k_all)
        v_all[...] = jnp.zeros_like(v_all)
        wqkv[:, :2 * HEAD_DIM] = wq_ref[...]
        wqkv[:, 2 * HEAD_DIM:3 * HEAD_DIM] = wk_ref[...]
        wqkv[:, 3 * HEAD_DIM:] = wv_ref[...]

    x = x_ref[...].astype(F32)
    inv = lax.rsqrt(jnp.mean(x * x, axis=-1, keepdims=True) + NORM_EPS)
    n = (x * inv * gain_ref[...].astype(F32)).astype(BF16)
    n_ref[...] = n
    qkv = dot(n, wqkv[...], (1, 0))
    cos_t, sin_t = rope_block(i, low_ref, high_ref)
    q0 = rotate(qkv[:, :HEAD_DIM], cos_t, sin_t).astype(BF16)
    q1 = rotate(qkv[:, HEAD_DIM:2 * HEAD_DIM], cos_t, sin_t).astype(BF16)
    k = rotate(qkv[:, 2 * HEAD_DIM:3 * HEAD_DIM], cos_t, sin_t).astype(BF16)
    v = qkv[:, 3 * HEAD_DIM:].astype(BF16)
    q_ref[:, :HEAD_DIM] = q0
    q_ref[:, HEAD_DIM:] = q1
    k_ref[...] = k
    v_ref[...] = v
    rows = pl.ds(pl.multiple_of(i * ROWS, ROWS), ROWS)
    k_all[rows, :] = k
    v_all[rows, :] = v

    def attend(c):
        hi = (c + 1) * WIDE
        lo = hi - WIDE
        q2 = jnp.concatenate([q0, q1], axis=0)
        row_id = lax.broadcasted_iota(jnp.int32, (2 * ROWS, WIDE), 0) % ROWS + (i * ROWS - lo)
        causal = row_id >= lax.broadcasted_iota(jnp.int32, (2 * ROWS, WIDE), 1)
        s_diag = jnp.where(causal, dot(q2, k_all[lo:hi, :], (1, 1)), MASK_VALUE)
        m = jnp.max(s_diag, axis=-1, keepdims=True)
        if lo:
            s_pre = dot(q2, k_all[:lo, :], (1, 1))
            m = jnp.maximum(m, jnp.max(s_pre, axis=-1, keepdims=True))
        p_diag = jnp.exp2((s_diag - m) * EXP2_SCALE)
        total = jnp.sum(p_diag, axis=-1, keepdims=True)
        if lo:
            p_pre = jnp.exp2((s_pre - m) * EXP2_SCALE)
            total = total + jnp.sum(p_pre, axis=-1, keepdims=True)
        scale = 1.0 / total
        o2 = dot((p_diag * scale).astype(BF16), v_all[lo:hi, :], (1, 0))
        if lo:
            o2 = o2 + dot((p_pre * scale).astype(BF16), v_all[:lo, :], (1, 0))
        o_ref[:, :HEAD_DIM] = o2[:ROWS].astype(BF16)
        o_ref[:, HEAD_DIM:] = o2[ROWS:].astype(BF16)

    for c in range(seq // WIDE):
        pl.when(i // (WIDE // ROWS) == c)(lambda c=c: attend(c))


def front(kv_index, x, gain, wq, wk, wv, low, high):
    seq, d = x.shape
    row = lambda w: pl.BlockSpec((ROWS, w), lambda i, kv: (i, 0))
    whole = lambda a: pl.BlockSpec(a.shape, lambda i, kv: (0,) * a.ndim)
    head = pl.BlockSpec((d, HEAD_DIM), lambda i, kv: (0, kv[0]))
    widths = (d, 2 * HEAD_DIM, HEAD_DIM, HEAD_DIM, 2 * HEAD_DIM)
    return pl.pallas_call(
        front_kernel,
        grid_spec=pltpu.PrefetchScalarGridSpec(
            num_scalar_prefetch=1, grid=(seq // ROWS,),
            in_specs=[row(d), whole(gain), whole(wq), head, head, whole(low), whole(high)],
            out_specs=[row(w) for w in widths],
            scratch_shapes=[pltpu.VMEM((d, 4 * HEAD_DIM), BF16), pltpu.VMEM((seq, HEAD_DIM), BF16), pltpu.VMEM((seq, HEAD_DIM), BF16)]),
        out_shape=[jax.ShapeDtypeStruct((seq, w), BF16) for w in widths],
        compiler_params=pltpu.CompilerParams(vmem_limit_bytes=48 * 2**20),
        cost_estimate=pl.CostEstimate(flops=2 * seq * d * 4 * HEAD_DIM + 4 * seq * seq * HEAD_DIM, bytes_accessed=5 * seq * d, transcendentals=seq * seq),
        name='front')(kv_index, x, gain, wq, wk, wv, low, high)


def attn_bwd_rows(i, do_both, q_ref, k_ref, v_ref, low_ref, high_ref, dq32, dk_acc, dv_acc):
    lo, hi = i * ROWS, (i + 1) * ROWS
    rows = pl.ds(lo, ROWS)
    causal = lax.broadcasted_iota(jnp.int32, (ROWS, ROWS), 0) <= lax.broadcasted_iota(jnp.int32, (ROWS, ROWS), 1)
    dk_acc[lo:hi, :] = jnp.zeros((ROWS, HEAD_DIM), F32)
    dv_acc[lo:hi, :] = jnp.zeros((ROWS, HEAD_DIM), F32)

    def one_head(head, carry):
        cols = pl.ds(pl.multiple_of(head * HEAD_DIM, HEAD_DIM), HEAD_DIM)
        q, do = q_ref[rows, cols], do_both[:, cols]
        k_all, v_all = k_ref[:hi, :], v_ref[:hi, :]
        s_t = dot(k_all, q, (1, 1))
        s_diag = jnp.where(causal, s_t[lo:], MASK_VALUE)
        s_t = jnp.concatenate([s_t[:lo], s_diag], axis=0) if lo else s_diag
        m = jnp.max(s_t, axis=0, keepdims=True)
        p = jnp.exp2((s_t - m) * EXP2_SCALE)
        p = p * (1.0 / jnp.sum(p, axis=0, keepdims=True))
        dp = dot(v_all, do, (1, 1))
        delta = jnp.sum(p * dp, axis=0, keepdims=True)
        ds = (p * (dp - delta) * SCORE_SCALE).astype(BF16)
        dv_acc[:hi, :] += dot(p.astype(BF16), do, (1, 0))
        dk_acc[:hi, :] += dot(ds, q, (1, 0))
        dq = dot(ds, k_all, (0, 0))
        cos_t, sin_t = rope_block(i, low_ref, high_ref)
        dq32[rows, cols] = rotate(dq, cos_t, -sin_t).astype(BF16).astype(F32)
        return carry

    lax.fori_loop(0, 2, one_head, 0)


SUBS = 2


def ring_kernel_setup(n):
    me = lax.axis_index('tp')
    chip, core = me // 2, me % 2
    right = (chip + 1) % n * 2 + core
    left = (chip + n - 1) % n * 2 + core
    sib = me + 1 - 2 * core
    barrier = pltpu.get_barrier_semaphore()
    for peer in (right, left, sib):
        pl.semaphore_signal(barrier, inc=1, device_id={'tp': peer}, device_id_type=pl.DeviceIdType.MESH)
    pl.semaphore_wait(barrier, 3)
    return chip, core, right, left, sib


def remote(src, dst, send, recv, peer):
    return pltpu.make_async_remote_copy(src_ref=src, dst_ref=dst, send_sem=send, recv_sem=recv,
                                        device_id={'tp': peer}, device_id_type=pl.DeviceIdType.MESH)


def ring_sum(n, place, extra, partial, finish, rider, gather_rider, out_ref, gain_acc, bufs, sems):
    chip, core, right, left, sib = place
    rs_buf, ag_buf, sib_buf, obuf = bufs
    rs_send, rs_recv, ag_send, ag_recv, sib_send, sib_recv, out_sem, credit = sems
    width = rs_buf.shape[-1]
    block = out_ref.shape[0] // n
    sub_rows = block // SUBS
    half = 2 * width
    peers = (right, left)

    def part(slot_ref, sub, with_extra):
        return slot_ref.at[pl.ds(sub * sub_rows, sub_rows + (extra if with_extra and sub == SUBS - 1 else 0)), :]

    def rs_copy(s, sub, way):
        return remote(part(rs_buf.at[way, s], sub, False), part(rs_buf.at[way, s + 1], sub, False),
                      rs_send.at[way, s, sub], rs_recv.at[way, s, sub], peers[way])

    def ag_copy(s, sub, way):
        return remote(part(ag_buf.at[way, s], sub, True), part(ag_buf.at[way, s + 1], sub, True),
                      ag_send.at[way, s, sub], ag_recv.at[way, s, sub], peers[way])

    def sib_copy(s, sub, way):
        rows = sub_rows + (extra if sub == SUBS - 1 else 0)
        k = SUBS * s + sub
        return remote(part(ag_buf.at[way, s], sub, True), sib_buf.at[way, k % 4, pl.ds(0, rows), :],
                      sib_send.at[way, k], sib_recv.at[way, k], sib)

    def my_part(dest, sub, way):
        row = pl.multiple_of(dest * block + sub * sub_rows, sub_rows)
        return partial(pl.ds(row, sub_rows), way)

    def dest_of(s, way):
        return (chip + n - 1 - s) % n if way == 0 else (chip + 1 + s) % n

    def local(ref, sub):
        return pl.ds(sub * sub_rows, sub_rows)

    for sub in range(SUBS):
        for way in range(2):
            rs_buf[way, 0, local(rs_buf, sub), :] = my_part(dest_of(0, way), sub, way)
            rs_copy(0, sub, way).start()
    rider(0)

    def rs_step(s, carry):
        for sub in range(SUBS):
            for way in range(2):
                rs_copy(s - 1, sub, way).wait_recv()
                rs_buf[way, s, local(rs_buf, sub), :] += my_part(dest_of(s, way), sub, way)
                rs_copy(s, sub, way).start()
            if sub == 0:
                rider(s)
        return carry

    lax.fori_loop(1, n - 1, rs_step, 0)
    for sub in range(SUBS):
        for way in range(2):
            rs_copy(n - 2, sub, way).wait_recv()
        finish(sub, [rs_buf[way, n - 1, local(rs_buf, sub), :] + my_part(chip, sub, way) for way in range(2)])

    def out_copy(whose, s, sub, way):
        b = (chip + n - s) % n if way == 0 else (chip + s) % n
        col = (core if whose == 0 else 1 - core) * half + way * width
        dst = out_ref.at[pl.ds(pl.multiple_of(b * block + sub * sub_rows, sub_rows), sub_rows), pl.ds(pl.multiple_of(col, 128), width)]
        return pltpu.make_async_copy(obuf.at[whose, sub, way], dst, out_sem.at[whose, sub, way])

    def emit(whose, s, sub, way, values):
        @pl.when(s >= 1)
        def _():
            out_copy(whose, s - 1, sub, way).wait()
        obuf[whose, sub, way] = values.astype(BF16)
        out_copy(whose, s, sub, way).start()

    def own_chunk(s, sub, forward):
        @pl.when(s >= 2)
        def _():
            pl.semaphore_wait(credit, 1)
        for way in range(2):
            if forward:
                ag_copy(s, sub, way).start()
            sib_copy(s, sub, way).start()
        for way in range(2):
            emit(0, s, sub, way, ag_buf[way, s, local(ag_buf, sub), :])
            if extra and sub == SUBS - 1:
                gain_acc[0, way] += ag_buf[way, s, pl.ds(block, extra), :]

    def sib_chunk(s, sub):
        k = SUBS * s + sub
        for way in range(2):
            sib_copy(s, sub, way).wait_recv()
            emit(1, s, sub, way, sib_buf[way, k % 4, pl.ds(0, sub_rows), :])
            if extra and sub == SUBS - 1:
                gain_acc[1, way] += sib_buf[way, k % 4, pl.ds(sub_rows, extra), :]

        @pl.when(s < n - 2)
        def _():
            pl.semaphore_signal(credit, inc=1, device_id={'tp': sib}, device_id_type=pl.DeviceIdType.MESH)

    own_chunk(0, 0, True)
    own_chunk(0, 1, True)
    rider(n - 1)
    sib_chunk(0, 0)

    def ag_step(s, carry):
        for sub in range(SUBS):
            for way in range(2):
                ag_copy(s - 1, sub, way).wait_recv()
            own_chunk(s, sub, True)
            if sub == 0:
                sib_chunk(s - 1, 1)
                gather_rider(s)
            else:
                sib_chunk(s, 0)
        return carry

    lax.fori_loop(1, n - 1, ag_step, 0)
    last = n - 1
    for sub in range(SUBS):
        for way in range(2):
            ag_copy(last - 1, sub, way).wait_recv()
        own_chunk(last, sub, False)
        if sub == 0:
            sib_chunk(last - 1, 1)
        else:
            sib_chunk(last, 0)
    sib_chunk(last, 1)
    for sub in range(SUBS):
        for way in range(2):
            for whose in range(2):
                out_copy(whose, last, sub, way).wait()

    def drain(s, carry):
        for sub in range(SUBS):
            for way in range(2):
                rs_copy(s, sub, way).wait_send()
                ag_copy(s, sub, way).wait_send()
                sib_copy(s, sub, way).wait_send()
        return carry

    lax.fori_loop(0, n - 1, drain, 0)
    for sub in range(SUBS):
        for way in range(2):
            sib_copy(last, sub, way).wait_send()


def ring_scratch(n, seq, d_model, extra):
    width, block = d_model // 4, seq // n
    sub_rows = block // SUBS
    dma = pltpu.SemaphoreType.DMA
    return [
        pltpu.VMEM((2, n, block, width), F32),
        pltpu.VMEM((2, n, block + extra, width), F32),
        pltpu.VMEM((2, 4, sub_rows + extra, width), F32),
        pltpu.VMEM((2, SUBS, 2, sub_rows, width), BF16),
        dma((2, n - 1, SUBS)), dma((2, n - 1, SUBS)), dma((2, n - 1, SUBS)), dma((2, n - 1, SUBS)),
        dma((2, SUBS * n)), dma((2, SUBS * n)), dma((2, SUBS, 2)), pltpu.SemaphoreType.REGULAR,
    ]


def out_kernel(n, o_ref, wo_ref, q_ref, k_ref, v_ref, low_ref, high_ref, x_ref, dout_ref,
               out_ref, dlhs_ref, lhs, rhs, x_rows, dout_rows, do_blk, dk_acc, x32, dkv32, wo32, o_got, wo_got, dq_got, dkv_got,
               row_sem, dout_sem, swap_send, swap_recv, *ring):
    bufs, sems = ring[:4], ring[4:]
    place = ring_kernel_setup(n)
    chip, core, right, left, sib = place
    width = bufs[0].shape[-1]
    half = 2 * width
    block = x_rows.shape[0]
    inner = o_ref.shape[1]
    count = q_ref.shape[0] // ROWS
    x_copy = pltpu.make_async_copy(
        x_ref.at[pl.ds(pl.multiple_of(chip * block, block), block), pl.ds(pl.multiple_of(core * half, 128), half)],
        x_rows, row_sem)

    def dout_copy(i):
        return pltpu.make_async_copy(dout_ref.at[pl.ds(i * ROWS, ROWS), :], dout_rows.at[i % 2], dout_sem.at[i % 2])

    swaps = [remote(src, dst, swap_send.at[k], swap_recv.at[k], sib)
             for k, (src, dst) in enumerate([(wo32, wo_got), (x32, o_got), (x32, dq_got), (dkv32, dkv_got)])]
    wo32[...] = wo_ref[:, pl.ds(pl.multiple_of((1 - core) * half, 128), half)].astype(F32)
    swaps[0].start()
    x32[...] = o_ref[...].astype(F32)
    swaps[1].start()
    x_copy.start()
    dout_copy(0).start()
    lhs[:, :inner] = o_ref[...]
    rhs[:inner, :] = wo_ref[:, pl.ds(pl.multiple_of(core * half, 128), half)]
    swaps[0].wait()
    rhs[inner:, :] = wo_got[...].astype(BF16)
    swaps[1].wait()
    lhs[:, inner:] = o_got[...].astype(BF16)

    def partial(rows, way):
        return dot(lhs[rows, :], rhs[:, way * width:(way + 1) * width], (1, 0))

    sub_rows = block // SUBS

    def finish(sub, sums):
        if sub == 0:
            x_copy.wait()
        for way in range(2):
            rows = pl.ds(sub * sub_rows, sub_rows)
            bufs[1][way, 0, rows, :] = sums[way] + x_rows[rows, way * width:(way + 1) * width].astype(F32)

    dv_acc = dkv32.at[:, pl.ds(HEAD_DIM, HEAD_DIM)]

    def ride(step):
        for i in range(step * count // n, (step + 1) * count // n):
            dout_copy(i).wait()
            if i + 1 < count:
                dout_copy(i + 1).start()
            do_blk[...] = dot(dout_rows[i % 2], wo_ref[...], (1, 1)).astype(BF16)
            attn_bwd_rows(i, do_blk, q_ref, k_ref, v_ref, low_ref, high_ref, x32, dk_acc, dv_acc)
        if step == n - 1:
            def turn_back(b, carry):
                rows = pl.ds(pl.multiple_of(b * ROWS, ROWS), ROWS)
                cos_t, sin_t = rope_block(b, low_ref, high_ref)
                dkv32[rows, :HEAD_DIM] = rotate(dk_acc[rows, :], cos_t, -sin_t)
                return carry
            lax.fori_loop(0, count, turn_back, 0)
            swaps[2].start()
            swaps[3].start()

    def rider(step):
        if isinstance(step, int):
            ride(step)
        else:
            for static in range(1, n - 1):
                pl.when(step == static)(lambda static=static: ride(static))

    def gather_rider(step):
        @pl.when(step == n // 2)
        def _():
            swaps[2].wait()
            swaps[3].wait()
            dlhs_ref[:, :inner] = x32[...].astype(BF16)
            dlhs_ref[:, inner:2 * inner] = (dkv32[...] + dkv_got[...]).astype(BF16)
            dlhs_ref[:, 2 * inner:] = dq_got[...].astype(BF16)

    ring_sum(n, place, 0, partial, finish, rider, gather_rider, out_ref, None, bufs, sems)


def grad_kernel(n, lhs, wqsib_ref, gain_ref, wq_ref, wk_ref, wv_ref, x_ref, dout_ref,
                out_ref, gsum_ref, rhs, gain, x_rows, dout_rows, unit_buf, stat_buf, gain_acc, row_sem, stat_send, stat_recv, *ring):
    bufs, sems = ring[:4], ring[4:]
    place = ring_kernel_setup(n)
    chip, core, right, left, sib = place
    width = bufs[0].shape[-1]
    block = x_rows.shape[0]
    inner = wq_ref.shape[1]
    half = 2 * width
    row = pl.multiple_of(chip * block, block)
    col = pl.multiple_of(core * half, 128)
    head_cols = pl.ds(pl.multiple_of(chip * HEAD_DIM, HEAD_DIM), HEAD_DIM)
    x_copy = pltpu.make_async_copy(x_ref.at[pl.ds(row, block), :], x_rows, row_sem.at[0])
    dout_copy = pltpu.make_async_copy(dout_ref.at[pl.ds(row, block), pl.ds(col, half)], dout_rows, row_sem.at[1])
    weights = [
        pltpu.make_async_copy(wq_ref.at[pl.ds(col, half), :], rhs.at[:, pl.ds(0, inner)], row_sem.at[2]),
        pltpu.make_async_copy(wk_ref.at[pl.ds(col, half), head_cols], rhs.at[:, pl.ds(inner, HEAD_DIM)], row_sem.at[3]),
        pltpu.make_async_copy(wv_ref.at[pl.ds(col, half), head_cols], rhs.at[:, pl.ds(inner + HEAD_DIM, HEAD_DIM)], row_sem.at[4]),
    ]
    for copy in weights + [x_copy, dout_copy]:
        copy.start()
    rhs[:, inner + 2 * HEAD_DIM:] = wqsib_ref[...].astype(BF16)
    gain[...] = gain_ref[:, pl.ds(col, half)].astype(F32)
    for copy in weights:
        copy.wait()
    gain_acc[...] = jnp.zeros_like(gain_acc)

    def partial(rows, way):
        return dot(lhs[rows, :], rhs[way * width:(way + 1) * width, :], (1, 1))

    sub_rows = block // SUBS

    def prepare(sub):
        rows = pl.ds(sub * sub_rows, sub_rows)
        x = x_rows[rows, :].astype(F32)
        inv = lax.rsqrt(jnp.mean(x * x, axis=-1, keepdims=True) + NORM_EPS)
        stat_buf[2, rows, :] = jnp.broadcast_to(inv, (sub_rows, HEAD_DIM))
        mine = x_rows[rows, pl.ds(col, half)].astype(F32)
        unit_buf[rows, :] = mine * inv

    def rider(step):
        if isinstance(step, int) and step == 0:
            x_copy.wait()
            dout_copy.wait()
            for sub in range(SUBS):
                prepare(sub)

    def stat_copy(sub):
        rows = pl.ds(sub * sub_rows, sub_rows)
        return remote(stat_buf.at[0, rows, :], stat_buf.at[1, rows, :], stat_send.at[sub], stat_recv.at[sub], sib)

    def finish(sub, sums):
        rows = pl.ds(sub * sub_rows, sub_rows)
        ag_buf = bufs[1]
        total = jnp.zeros((sub_rows, 1), F32)
        for way in range(2):
            cols = slice(way * width, (way + 1) * width)
            unit = unit_buf[rows, cols]
            prod = sums[way] * unit
            total = total + jnp.sum(prod * gain[:, cols], axis=-1, keepdims=True)
            gsum = jnp.sum(prod.reshape(sub_rows // 8, 8, width), axis=0)
            ag_buf[way, 0, pl.ds(block, 8), :] = gsum if sub == 0 else gsum + ag_buf[way, 0, pl.ds(block, 8), :]
            ag_buf[way, 0, rows, :] = sums[way]
        stat_buf[0, rows, :] = jnp.broadcast_to(total, (sub_rows, HEAD_DIM))
        stat_copy(sub).start()
        stat_copy(sub).wait()
        mean = (stat_buf[0, rows, 0:1] + stat_buf[1, rows, 0:1]) * (1.0 / (2 * half))
        inv = stat_buf[2, rows, 0:1]
        for way in range(2):
            cols = slice(way * width, (way + 1) * width)
            scaled = ag_buf[way, 0, rows, :] * gain[:, cols]
            ag_buf[way, 0, rows, :] = dout_rows[rows, cols].astype(F32) + inv * (scaled - unit_buf[rows, cols] * mean)

    ring_sum(n, place, 8, partial, finish, rider, lambda step: None, out_ref, gain_acc, bufs, sems)
    for way in range(2):
        gsum_ref[core, way] = jnp.sum(gain_acc[0, way], axis=0, keepdims=True)
        gsum_ref[1 - core, way] = jnp.sum(gain_acc[1, way], axis=0, keepdims=True)


def final_kernel(n_ref, dout_ref, o_ref, d_ref, out_in, gh_in, out_ref, gh_ref, wq_ref, wk_ref, wv_ref, wo_ref):
    inner = o_ref.shape[1]
    out_ref[...] = out_in[...]
    gh_ref[...] = gh_in[...]
    dw = dot(n_ref[...], d_ref[:, :2 * inner], (0, 0))
    wq_ref[...] = dw[:, :inner]
    wk_ref[...] = dw[:, inner:inner + HEAD_DIM]
    wv_ref[...] = dw[:, inner + HEAD_DIM:]
    wo_ref[...] = dot(o_ref[...], dout_ref[...], (0, 0))


def final(n, dout, o, dlhs, out, gh):
    seq, d = n.shape
    inner = o.shape[1]
    col = pl.BlockSpec((seq, ROWS), lambda j: (0, j))
    whole = lambda a: pl.BlockSpec(a.shape, lambda j: (0, 0))
    row = lambda w: pl.BlockSpec((ROWS, w), lambda j: (j, 0))
    shape = jax.ShapeDtypeStruct
    return pl.pallas_call(
        final_kernel, grid=(d // ROWS,),
        in_specs=[col, col, whole(o), whole(dlhs), col, col],
        out_specs=[col, col, row(inner), row(HEAD_DIM), row(HEAD_DIM), pl.BlockSpec((inner, ROWS), lambda j: (0, j))],
        out_shape=[shape(out.shape, BF16), shape(gh.shape, BF16), shape((d, inner), F32), shape((d, HEAD_DIM), F32),
                   shape((d, HEAD_DIM), F32), shape((inner, d), F32)],
        compiler_params=pltpu.CompilerParams(vmem_limit_bytes=48 * 2**20),
        cost_estimate=pl.CostEstimate(flops=6 * seq * inner * d, bytes_accessed=14 * seq * d, transcendentals=0),
        name='final')(n, dout, o, dlhs, out, gh)


def out_sum(n, o, wo, q, k, v, low, high, x, dout):
    seq, d_model = x.shape
    half, block, inner = d_model // 2, seq // n, o.shape[1]
    vmem, hbm = pl.BlockSpec(memory_space=pltpu.VMEM), pl.BlockSpec(memory_space=pl.ANY)
    shape = jax.ShapeDtypeStruct
    dma = pltpu.SemaphoreType.DMA
    rows32 = pltpu.VMEM((seq, inner), F32)
    wide32 = pltpu.VMEM((inner, half), F32)
    return pl.pallas_call(
        functools.partial(out_kernel, n),
        out_shape=[shape((seq, d_model), BF16), shape((seq, 2 * inner + 2 * HEAD_DIM), BF16)],
        in_specs=[vmem] * 7 + [hbm] * 2, out_specs=[hbm, vmem],
        scratch_shapes=[pltpu.VMEM((seq, 2 * inner), BF16), pltpu.VMEM((2 * inner, half), BF16),
                        pltpu.VMEM((block, half), BF16), pltpu.VMEM((2, ROWS, d_model), BF16), pltpu.VMEM((ROWS, inner), BF16),
                        pltpu.VMEM((seq, HEAD_DIM), F32), rows32, rows32, wide32, rows32, wide32, rows32, rows32,
                        dma, dma((2,)), dma((4,)), dma((4,))]
        + ring_scratch(n, seq, d_model, 0),
        compiler_params=pltpu.CompilerParams(collective_id=1, has_side_effects=True, vmem_limit_bytes=VMEM_LIMIT),
        cost_estimate=pl.CostEstimate(flops=10 * seq * seq * HEAD_DIM, bytes_accessed=4 * seq * d_model, transcendentals=seq * seq),
        name='out_sum')(o, wo, q, k, v, low, high, x, dout)


def grad_sum(n, dlhs, wq_sib, gain, wq, wk, wv, x, dout):
    seq, d_model = x.shape
    half, block, width = d_model // 2, seq // n, d_model // 4
    kdim = dlhs.shape[1]
    vmem, hbm = pl.BlockSpec(memory_space=pltpu.VMEM), pl.BlockSpec(memory_space=pl.ANY)
    shape = jax.ShapeDtypeStruct
    dma = pltpu.SemaphoreType.DMA
    return pl.pallas_call(
        functools.partial(grad_kernel, n),
        out_shape=[shape((seq, d_model), BF16), shape((2, 2, 1, width), F32)],
        in_specs=[vmem] * 3 + [hbm] * 5, out_specs=[hbm, vmem],
        scratch_shapes=[pltpu.VMEM((half, kdim), BF16), pltpu.VMEM((1, half), F32),
                        pltpu.VMEM((block, d_model), BF16), pltpu.VMEM((block, half), BF16), pltpu.VMEM((block, half), F32),
                        pltpu.VMEM((3, block, HEAD_DIM), F32), pltpu.VMEM((2, 2, 8, width), F32),
                        dma((5,)), dma((SUBS,)), dma((SUBS,))]
        + ring_scratch(n, seq, d_model, 8),
        compiler_params=pltpu.CompilerParams(collective_id=2, has_side_effects=True, vmem_limit_bytes=VMEM_LIMIT),
        cost_estimate=pl.CostEstimate(flops=4 * seq * kdim * half, bytes_accessed=4 * seq * d_model, transcendentals=0),
        name='grad_sum')(dlhs, wq_sib, gain, wq, wk, wv, x, dout)


def solution(mesh):
    tp_size = mesh.shape['tp']
    chips = tp_size // 2
    swap = [(source, source ^ 1) for source in range(tp_size)]

    def block_fn(hidden, grad_out, norm_gain, w_query, w_key, w_value, w_out):
        batch, seq_len, d_model = hidden.shape
        half = d_model // 2
        tp_index = lax.axis_index('tp')
        kv_index, core = tp_index // 2, tp_index % 2
        low, high = rope_tables(seq_len // ROWS)
        x, dout = hidden[0], grad_out[0]
        gain = norm_gain[None, :]
        wq_sib = lax.ppermute(lax.dynamic_slice_in_dim(w_query, (1 - core) * half, half, axis=0).astype(F32), 'tp', swap)
        n, q, k, v, o = front(kv_index[None], x, gain, w_query, w_key, w_value, low, high)
        out, dlhs = out_sum(chips, o, w_out, q, k, v, low, high, x, dout)
        gh, gain_sum = grad_sum(chips, dlhs, wq_sib, gain, w_query, w_key, w_value, x, dout)
        out, gh, grad_w_query, grad_w_key, grad_w_value, grad_w_out = final(n, dout, o, dlhs, out, gh)
        return out[None], gh[None], gain_sum.reshape(-1), grad_w_query, grad_w_key, grad_w_value, grad_w_out

    act_spec = P('dp', None, None)
    return jax.shard_map(
        block_fn, mesh=mesh,
        in_specs=(act_spec, act_spec, P(None), P(None, 'tp'), P(None, None), P(None, None), P('tp', None)),
        out_specs=(act_spec, act_spec, P('dp'), P('dp', 'tp'), P('dp', 'tp'), P('dp', 'tp'), P(('dp', 'tp'), None)),
        check_vma=False)
```

time: 543 us -> 514 us (0.947); the launches traced: 532 us -> 514 us
  Pallas kernels: 464 us -> 495 us
  matrix products: 25.4 us -> 0 us
  local copies, waits for them, and re-layouts: 29.2 us -> 10.9 us
    pallas_call x3, Pallas kernels: 246 us -> 277 us  [the longest x1 221 us: out_sum(): pl.pallas_call(functools.partial(out_kernel, n), out_shape=[shape((seq, d...]
    dot_general x4 -> x0, matrix products: 25.4 us -> none  [dot(): lax.dot_general(a, b, ((contract[:1], contract[1:]), ((), ())), preferred...]
    unnamed x28 -> x20, local copies, waits for them, and re-layouts: 22.8 us -> 9.6 us
  transfers between devices with their start and end apart: 5 -> 1, of which waited for: 0 -> 0; matrix products, arithmetic and copies ran while one was open for 6% -> 0% of each run, Pallas kernels for 41% -> 49%
where the time goes in v3:
time: 514 us
  Pallas kernels  495 us (96%)
  local copies, waits for them, and re-layouts  10.9 us (2%)
    pallas_call x1, Pallas kernels, out_sum(): pl.pallas_call(functools.partial(out_kernel, n), out_shape=[shape((seq, d...  221 us
    pallas_call x1, Pallas kernels, grad_sum(): pl.pallas_call(functools.partial(grad_kernel, n), out_shape=[shape((seq,...  217 us
    pallas_call x1, Pallas kernels, front(): pl.pallas_call(front_kernel, grid_spec=pltpu.PrefetchScalarGridSpec(num_s...  29.9 us
    pallas_call x1, Pallas kernels, final(): pl.pallas_call(final_kernel, grid=(d // ROWS,), in_specs=[col, col, whole...  26.9 us
  transfers between devices with their start and end apart: 1, of which 0 were waited for; matrix products, arithmetic and copies ran while one was open for 0% of the time, Pallas kernels for 49%

profile of v3, /device:TPU:21, one launch (start us, length us, event | category | flops | bytes accessed | tf_op | source)
XLA Modules:
  0.0 513.9 jit_solution(9395498698263625862)
XLA Ops:
  0.6 2.2 dynamic-slice_convert_fusion
  2.9 4.7 collective-permute-start
  7.6 0.7 broadcast_in_dim.13.gain_ref
  8.3 0.0 copy-start.8
  8.3 0.0 copy-start.3
  8.3 1.3 copy-done.3
  9.6 0.0 copy-start.7
  9.6 0.9 copy-done.7
  10.5 0.0 copy-start.9
  10.5 0.7 copy-done.9
  11.2 29.9 %front.1 = (bf16[2048,2560]{1,0:T(8,128)(2,1)}, bf16[2048,256]{1,0:T(8,128)(2,1)S(1)}, bf16[2048,128]{1,0:T(8,128)(2,1)S(1)}, bf16[2048,128]{1,0:T(8,128)(2,1)S(1)}, bf16[2048,256]{1,0:T(8,128)(2,1)S(1)}) custom-call(s32[1]{0:T(128)} %bitcast.kv_ref, bf16[2048,2560]{1,0:T(8,128)(2,1)} %bitcast.8, bf16[1,2560]{1,0:T(2,128)(2,1)S(1)} %broadcast_in_dim.13.gain_ref, ...), custom_call_target="tpu_custom_call" | custom-call | flops 7516192768 | bytes 26214400 | tf_op jit(solution)/shard_map/front/pallas_call | solution.py:114
  41.1 0.0 copy-done.8
  41.1 0.0 copy-start.1
  41.1 1.0 copy-done.1
  42.1 0.0 copy-start.4
  42.1 1.0 copy-done.4
  43.0 0.0 copy-start.5
  43.0 0.8 copy-done.5
  43.8 0.0 copy-start.6
  43.8 0.8 copy-done.6
  44.6 220.6 %out_sum.1 = (bf16[2048,2560]{1,0:T(8,128)(2,1)}, bf16[2048,768]{1,0:T(8,128)(2,1)}) custom-call(bf16[2048,256]{1,0:T(8,128)(2,1)} %copy-done.1, bf16[256,2560]{1,0:T(8,128)(2,1)} %wo_ref.1, bf16[2048,256]{1,0:T(8,128)(2,1)} %copy-done.4, bf16[2048,128]{1,0:T(8,128)(2,1)} %copy-done.5, bf16[2048,128]{1,0:T(8,128)(2,1)} %copy-done.6, ...), custom_call_target="tpu_custom_call" | custom-call | flops 5368709120 | bytes 20971520 | tf_op jit(solution)/shard_map/out_sum/pallas_call | solution.py:535
  265.2 0.0 collective-permute-done.wqsib_ref
  265.3 217.2 %grad_sum.1 = (bf16[2048,2560]{1,0:T(8,128)(2,1)}, f32[2,2,1,640]{3,2,1,0:T(1,128)}) custom-call(bf16[2048,768]{1,0:T(8,128)(2,1)} %get-tuple-element.27.lhs.d_ref, f32[1280,256]{1,0:T(8,128)} %collective-permute-done.wqsib_ref, bf16[1,2560]{1,0:T(2,128)(2,1)} %copy-done.8, bf16[2560,256]{1,0:T(8,128)(2,1)} %wq_ref.3, bf16[2560,1024]{1,0:T(8,128)(2,1)} %wk_ref.3, ...), custom_call_target="tpu_custom_call" | custom-call | flops 8053063680 | bytes 20971520 | tf_op jit(solution)/shard_map/grad_sum/pallas_call | solution.py:556
  482.4 0.7 reduce
  483.2 0.6 reshape.17
  483.8 0.0 copy-start
  483.8 1.9 copy-done
  485.7 0.0 copy-start.2
  485.7 1.2 copy-done.2
  486.9 26.9 %final.1 = (bf16[2048,2560]{1,0:T(8,128)(2,1)}, bf16[2048,2560]{1,0:T(8,128)(2,1)}, f32[2560,256]{1,0:T(8,128)}, f32[2560,128]{1,0:T(8,128)}, f32[2560,128]{1,0:T(8,128)}, /*index=5*/f32[256,2560]{1,0:T(8,128)}) custom-call(bf16[2048,2560]{1,0:T(8,128)(2,1)} %get-tuple-element.22.n_ref, bf16[2048,2560]{1,0:T(8,128)(2,1)} %bitcast.7, ...), custom_call_target="tpu_custom_call" | custom-call | flops 8053063680 | bytes 73400320 | tf_op jit(solution)/shard_map/final/pallas_call | solution.py:516
Async XLA Ops:
  2.9 262.4 %collective-permute-start = (f32[1280,256]{1,0:T(8,128)}, f32[1280,256]{1,0:T(8,128)}, u32[]{:S(2)}, u32[]{:S(2)}) collective-permute-start(f32[1280,256]{1,0:T(8,128)} %dynamic-slice_convert_fusion), channel_id=1, source_target_pairs={{0,1},{1,0},{2,3},{3,2},{4,5},{5,4},{6,7},{7,6},{8,9},{9,8},{10,11... | collective-permute-start | bytes 3932168 | tf_op jit(solution)/shard_map/ppermute | solution.py:583
  8.3 32.9 %copy-start.8 = (bf16[1,2560]{1,0:T(2,128)(2,1)}, bf16[1,2560]{1,0:T(2,128)(2,1)S(1)}, u32[]{:S(2)}) copy-start(bf16[1,2560]{1,0:T(2,128)(2,1)S(1)} %broadcast_in_dim.13.gain_ref) | copy-start | bytes 15364
  8.3 1.3 copy-start.3
  9.6 0.9 copy-start.7
  10.5 0.7 copy-start.9
  41.1 1.0 copy-start.1
  42.1 1.0 copy-start.4
  43.0 0.8 copy-start.5
  43.8 0.8 copy-start.6
  483.8 1.9 copy-start
  485.7 1.2 copy-start.2
